TPU v7x, 16 devices: a 4x2x1 block of a 4x4x8 slice. The times are simulated.
16 devices in a mesh: dp: 2 (over y, z), dcp: 8 (over x, core).
Axes of the slice: x: 4, y: 2, z: 1, core: 2. Of those that a mesh axis runs over, the one named last changes fastest.
The devices are a block of a 4x4x8 slice.
Arguments:
- q: bfloat16 [256, 16, 576], P('dp', 'dcp'), parts along dimension 0
- cache: bfloat16 [256, 32, 8, 8, 576], P('dp', None, 'dcp'), parts along dimension 0
- lens: int32 [256], P('dp'), parts along dimension 0
Outputs:
- output: bfloat16 [256, 16, 512], P('dp', 'dcp'), parts along dimension 0
There are 2 independent parts. A program takes and returns all parts, laid end to end along the dimension named above; each array names one.
All inputs are finite; a program needn't handle non-finite values.
Results may differ from a plain program's by a relative error of at most 0.0081033.
Values are sent between devices in bfloat16 or wider.
A program may use at most 768 MiB of HBM per device.

v0:
```python
import jax
import jax.numpy as jnp
from jax import lax
from jax.sharding import PartitionSpec as P

ROPE = 64
QK_DIM = 192
SCALE = QK_DIM ** -0.5


def solution(mesh):
    n = mesh.shape['dcp']

    def local(q, cache, lens):
        b, hl, k = q.shape
        r = cache.shape[1]
        page = cache.shape[3]
        lorav = k - ROPE
        d = lax.axis_index('dcp')
        qa = lax.all_gather(q, 'dcp', axis=1, tiled=True)
        c = cache.reshape(b, r * page, k)
        pos = (jnp.arange(r)[:, None] * n + d) * page + jnp.arange(page)[None, :]
        valid = pos.reshape(r * page)[None, :] < lens[:, None]
        s = jnp.einsum('bhk,btk->bht', qa, c, preferred_element_type=jnp.float32) * SCALE
        s = jnp.where(valid[:, None, :], s, -jnp.inf)
        m = jnp.max(s, axis=2)
        m = jnp.where(jnp.isfinite(m), m, 0.0)
        p = jnp.exp(s - m[:, :, None])
        l = jnp.sum(p, axis=2)
        has = l > 0.0
        lsafe = jnp.where(has, l, 1.0)
        pv = jnp.einsum('bht,btk->bhk', p.astype(jnp.bfloat16), c[:, :, :lorav], preferred_element_type=jnp.float32)
        od = (pv / lsafe[:, :, None]).astype(jnp.bfloat16)
        lse = jnp.where(has, m + jnp.log(lsafe), -jnp.inf)
        od = lax.all_to_all(od.reshape(b, n, hl, lorav), 'dcp', 1, 1, tiled=True)
        lse = lax.all_to_all(lse.reshape(b, n, hl), 'dcp', 1, 1, tiled=True)
        top = jnp.max(lse, axis=1)
        w = jnp.exp(lse - top[:, None, :])
        o = jnp.sum(w[:, :, :, None] * od.astype(jnp.float32), axis=1) / jnp.sum(w, axis=1)[:, :, None]
        return o.astype(jnp.bfloat16)

    return jax.shard_map(local, mesh=mesh, in_specs=(P('dp', 'dcp', None), P('dp', None, 'dcp', None, None), P('dp')), out_specs=P('dp', 'dcp', None), check_vma=False)
```

profile of v0, /device:TPU:112, one launch (start us, length us, event | category | flops | bytes accessed | tf_op | source)
XLA Modules:
  0.0 153.3 jit_solution(3444747796998845844)
XLA Ops:
  6.5 0.0 all-gather.2.cloned.1.call-start
  6.6 0.7 all-gather.2.cloned.1.call-update
  7.3 0.1 iota_add_fusion
  7.4 0.1 add.40
  7.5 0.0 copy-start.1
  7.5 51.3 %copy.13 = bf16[128,32,1,8,576]{4,3,1,0,2:T(8,128)(2,1)} copy(bf16[128,32,1,8,576]{0,4,3,2,1:T(8,128)(2,1)} %param.4) | data formatting | bytes 75497472 | tf_op args[1]
  58.8 0.1 broadcast_compare_fusion
  58.9 0.0 all-gather.2.cloned.1.call-done
  58.9 3.9 %copy.14 = bf16[128,16,576]{2,1,0:T(8,128)(2,1)S(1)} copy(bf16[128,16,576]{0,2,1:T(8,128)(2,1)} %all-gather.2.cloned.1.call-done) | data formatting | bytes 4718592 | tf_op jit(solution)/shard_map/all_gather | solution.py:20
  62.8 19.1 %fusion.2 = (f32[128,16]{1,0:T(8,128)S(1)}, f32[128,16,256]{2,1,0:T(8,128)}) fusion(pred[128,256]{1,0:T(8,128)(4,1)S(1)} %broadcast_compare_fusion, bf16[128,16,576]{2,1,0:T(8,128)(2,1)S(1)} %copy.14, bf16[128,32,1,8,576]{4,3,1,0,2:T(8,128)(2,1)} %copy.13), kind=kOutput, calls=%fused_computation.6 | convolution fusion | flops 605550592 | bytes 42246144 | tf_op jit(solution)/shard_map/bhk,btk->bht/dot_general | solution.py:24
  82.0 2.6 %fusion.4 = f32[128,16]{1,0:T(8,128)S(1)} fusion(f32[128,16,256]{2,1,0:T(8,128)} %get-tuple-element.8, f32[128,16]{1,0:T(8,128)S(1)} %is-finite_select_fusion, pred[128,256]{1,0:T(8,128)(4,1)S(1)} %broadcast_compare_fusion), kind=kLoop, calls=%fused_computation.8 | loop fusion | flops 2095104 | bytes 2146304 | tf_op jit(solution)/shard_map/reduce_sum | solution.py:29
  84.5 0.1 copy.16
  84.6 0.6 compare_select_fusion.1
  85.2 5.3 %all-to-all-start = ((f32[128,8,2]{0,2,1:T(2,128)}), f32[128,8,2]{0,2,1:T(2,128)S(1)}, u32[]{:S(2)}, u32[]{:S(2)}) async-start(f32[128,8,2]{0,2,1:T(2,128)} %compare_select_fusion.1), calls=%async_computation | async-start | bytes 16384 | tf_op jit(solution)/shard_map/all_to_all | solution.py:36
  90.6 14.4 %divide_convert_fusion = bf16[128,16,512]{2,1,0:T(8,128)(2,1)} fusion(f32[128,16]{1,0:T(8,128)S(1)} %compare_select_fusion, bf16[128,256,576]{2,1,0:T(8,128)(2,1)} %bitcast.8, f32[128,16,256]{2,1,0:T(8,128)S(1)} %copy-done, f32[128,16]{1,0:T(8,128)S(1)} %is-finite_select_fusion, pred[128,256]{1,0:T(8,128)(4,1)S(1)} %broadcast_compare_fusion), kind=kOutput, calls=%fused_computation.3 | convolution fusion | flops 541065216 | bytes 37797888 | tf_op jit(solution)/shard_map/bht,btk->bhk/dot_general | solution.py:32
  105.0 2.7 %reshape.67 = bf16[128,8,2,512]{3,2,1,0:T(2,128)(2,1)S(1)} reshape(bf16[128,16,512]{2,1,0:T(8,128)(2,1)} %divide_convert_fusion) | data formatting | bytes 4194304 | tf_op jit(solution)/shard_map/reshape | solution.py:35
  107.7 3.0 %copy.19 = bf16[128,8,2,512]{3,2,0,1:T(2,128)(2,1)} copy(bf16[128,8,2,512]{3,2,1,0:T(2,128)(2,1)S(1)} %reshape.67) | data formatting | bytes 4194304 | tf_op jit(solution)/shard_map/reshape | solution.py:35
  110.7 0.0 all-to-all-done
  110.7 4.8 %all-to-all-start.1 = ((bf16[128,8,2,512]{3,2,0,1:T(2,128)(2,1)}), bf16[128,8,2,512]{3,2,0,1:T(2,128)(2,1)S(1)}, u32[]{:S(2)}, u32[]{:S(2)}) async-start(bf16[128,8,2,512]{3,2,0,1:T(2,128)(2,1)} %copy.19), calls=%async_computation.1 | async-start | bytes 4194304 | tf_op jit(solution)/shard_map/all_to_all | solution.py:35
  115.5 0.1 copy.20
  115.7 0.2 copy.18
  115.9 26.8 %all-to-all-done.1 = bf16[128,8,2,512]{3,2,0,1:T(2,128)(2,1)S(1)} async-done(((bf16[128,8,2,512]{3,2,0,1:T(2,128)(2,1)}), bf16[128,8,2,512]{3,2,0,1:T(2,128)(2,1)S(1)}, u32[]{:S(2)}, u32[]{:S(2)}) %all-to-all-start.1) | async-done | bytes 2097184 | tf_op jit(solution)/shard_map/all_to_all | solution.py:35
  142.7 2.8 %multiply_reduce_fusion = f32[128,2,512]{2,1,0:T(2,128)S(1)} fusion(bf16[128,8,2,512]{3,2,0,1:T(2,128)(2,1)S(1)} %all-to-all-done.1, f32[128,8,2]{2,0,1:T(8,128)S(1)} %copy.18), kind=kLoop, calls=%fused_computation.2 | loop fusion | flops 3014656 | bytes 2629632 | tf_op jit(solution)/shard_map/reduce_sum | solution.py:39
  145.4 1.0 divide_convert_fusion.1
  (9 shorter events, 0.1 us)
Async XLA Ops:
  6.5 52.3 %all-gather.2.cloned.1.call-start = ((), (), s32[]{:S(2)}) async-start(), calls=%async_computation.2 | async-start | bytes 2654208 | tf_op jit(solution)/shard_map/all_gather | solution.py:20
  7.5 51.3 %copy-start.1 = (s32[128]{0:T(128)S(1)}, s32[128]{0:T(128)}, u32[]{:S(2)}) copy-start(s32[128]{0:T(128)} %param.5) | copy-start | bytes 1540
  81.9 8.7 %copy-start = (f32[128,16,256]{2,1,0:T(8,128)S(1)}, f32[128,16,256]{2,1,0:T(8,128)}, u32[]{:S(2)}) copy-start(f32[128,16,256]{2,1,0:T(8,128)} %get-tuple-element.8) | copy-start | bytes 6291460
  85.2 25.4 %all-to-all-start = ((f32[128,8,2]{0,2,1:T(2,128)}), f32[128,8,2]{0,2,1:T(2,128)S(1)}, u32[]{:S(2)}, u32[]{:S(2)}) async-start(f32[128,8,2]{0,2,1:T(2,128)} %compare_select_fusion.1), calls=%async_computation | async-start | bytes 16384 | tf_op jit(solution)/shard_map/all_to_all | solution.py:36
  110.7 32.0 %all-to-all-start.1 = ((bf16[128,8,2,512]{3,2,0,1:T(2,128)(2,1)}), bf16[128,8,2,512]{3,2,0,1:T(2,128)(2,1)S(1)}, u32[]{:S(2)}, u32[]{:S(2)}) async-start(bf16[128,8,2,512]{3,2,0,1:T(2,128)(2,1)} %copy.19), calls=%async_computation.1 | async-start | bytes 4194304 | tf_op jit(solution)/shard_map/all_to_all | solution.py:35
Sparse Core Ops, SparseCore 0:
  8.9 24.5 all-gather.1
where the time goes:
time: 155 us; the launch traced here: 153 us
  local copies, waits for them, and re-layouts  61.4 us (40%)
  matrix products  33.5 us (22%)
  waiting for transfers between devices  27.6 us (18%)
  between operations  13.5 us (9%)
  starting transfers between devices  10.1 us (7%)
  other arithmetic  7.15 us (5%)
    unnamed x5, local copies, waits for them, and re-layouts  51.3 us
    all_to_all x1, waiting for transfers between devices, local(): od = lax.all_to_all(od.reshape(b, n, hl, lorav), 'dcp', 1, 1, tiled=True)  26.8 us
    dot_general x1, matrix products, local(): jnp.einsum('bhk,btk->bht', qa, c, preferred_element_type=jnp.float32)  19.1 us
    dot_general x1, matrix products, local(): jnp.einsum('bht,btk->bhk', p.astype(jnp.bfloat16), c[:, :, :lorav], prefe...  14.4 us
    reshape x2, local copies, waits for them, and re-layouts, local(): od = lax.all_to_all(od.reshape(b, n, hl, lorav), 'dcp', 1, 1, tiled=True)  5.72 us
    all_to_all x1, starting transfers between devices, local(): lse = lax.all_to_all(lse.reshape(b, n, hl), 'dcp', 1, 1, tiled=True)  5.3 us
    all_to_all x1, starting transfers between devices, local(): od = lax.all_to_all(od.reshape(b, n, hl, lorav), 'dcp', 1, 1, tiled=True)  4.81 us
    all_gather x1, local copies, waits for them, and re-layouts, local(): qa = lax.all_gather(q, 'dcp', axis=1, tiled=True)  3.92 us
  transfers between devices with their start and end apart: 3, of which 1 were waited for; matrix products, arithmetic and copies ran while one was open for 47% of the time, Pallas kernels for 0%

commit v1 on v0

v1 whole, which is shorter than its diff:
```python
import functools
import jax
import jax.numpy as jnp
from jax import lax
from jax.experimental import pallas as pl
from jax.experimental.pallas import tpu as pltpu
from jax.sharding import PartitionSpec as P

ROPE = 64
QK_DIM = 192
SCALE = QK_DIM ** -0.5
LOG2E = 1.4426950408889634
KP = 640
TB = 64


def kernel(n, lm_ref, q_ref, c_hbm, o_ref, lse_ref, stage, y, qt, s_ref, sems):
    d = lax.axis_index('dcp')
    nr, page, k, b = c_hbm.shape
    g = y.shape[1]
    t = nr * page
    lora = k - ROPE

    def fetch(r, slot):
        return pltpu.make_async_copy(c_hbm.at[r], stage.at[slot], sems.at[slot])

    for i in range(2):
        fetch(i, i).start()

    def load(r, _):
        slot = lax.rem(r, 3)

        @pl.when(r + 2 < nr)
        def _():
            fetch(r + 2, lax.rem(r + 2, 3)).start()

        fetch(r, slot).wait()
        for p in range(page):
            x = stage[slot, p]
            xt = jnp.concatenate([x, jnp.zeros((KP - k, b), x.dtype)], 0).T
            y[r * page + p] = xt.reshape(g, b // g, KP)
        return 0

    lax.fori_loop(0, nr, load, 0)

    tl = lax.broadcasted_iota(jnp.int32, (TB, 1, 1), 0)

    def group(gi, _):
        qt[...] = q_ref[gi].T

        def qk(j, m):
            lhs = y[pl.ds(j * TB, TB), gi].reshape(TB * 16, KP)
            s = jnp.dot(lhs, qt[...], preferred_element_type=jnp.float32)
            s = s.reshape(TB, 2, 8, 256)
            ti = tl + j * TB
            pos = ((ti // page) * n + d) * page + lax.rem(ti, page)
            out = []
            for o in range(2):
                so = s[:, o, :, o * 128:(o + 1) * 128] * (SCALE * LOG2E)
                so = jnp.where(pos < lm_ref[gi, o][None], so, -jnp.inf)
                s_ref[o, pl.ds(j * TB, TB)] = so
                out.append(jnp.maximum(m[o], jnp.max(so, axis=0)))
            return tuple(out)

        m = lax.fori_loop(0, t // TB, qk, (jnp.full((8, 128), -jnp.inf, jnp.float32),) * 2)
        m = [jnp.max(x, axis=0, keepdims=True) for x in m]
        m = [jnp.where(x == -jnp.inf, 0.0, x) for x in m]
        lane = lax.broadcasted_iota(jnp.int32, (128, TB * 16), 1)
        first = lax.rem(lane, 16) < 8

        def pv(j, carry):
            l, acc = carry
            ps = []
            ls = []
            for o in range(2):
                p = jnp.exp2(s_ref[o, pl.ds(j * TB, TB)] - m[o][None])
                ls.append(l[o] + jnp.sum(p, axis=0))
                ps.append(p)
            pm = jnp.concatenate(ps, axis=1).astype(jnp.bfloat16).reshape(TB * 16, 128).T
            z = jnp.zeros_like(pm)
            pt = jnp.concatenate([jnp.where(first, pm, z), jnp.where(first, z, pm)], axis=0)
            v = y[pl.ds(j * TB, TB), gi, :, 0:lora].reshape(TB * 16, lora)
            acc = acc + jnp.dot(pt, v, preferred_element_type=jnp.float32)
            return tuple(ls), acc

        l, acc = lax.fori_loop(0, t // TB, pv, ((jnp.zeros((8, 128), jnp.float32),) * 2, jnp.zeros((256, lora), jnp.float32)))
        for o in range(2):
            lo = jnp.sum(l[o], axis=0, keepdims=True)
            has = lo > 0.0
            lsafe = jnp.where(has, lo, 1.0)
            lse_ref[gi, o:o + 1] = jnp.where(has, m[o] + jnp.log2(lsafe), -jnp.inf)
            col = jnp.broadcast_to(1.0 / lsafe, (8, 128)).T[:, 0:1]
            o_ref[gi, o] = (acc[o * 128:(o + 1) * 128] * col).astype(jnp.bfloat16)
        return 0

    lax.fori_loop(0, g, group, 0)


def solution(mesh):
    n = mesh.shape['dcp']

    def local(q, cache, lens):
        b, hl, k = q.shape
        nr, page = cache.shape[1], cache.shape[3]
        lora = k - ROPE
        g = b // 16
        h = n * hl
        qa = lax.all_gather(q, 'dcp', axis=0)
        qa = jnp.pad(qa.reshape(n, g, 2, 8, hl, k), [(0, 0)] * 5 + [(0, KP - k)])
        qa = qa.transpose(1, 2, 0, 3, 4, 5).reshape(g, 256, KP)
        lane = jnp.arange(128)
        diag = (lane[None, :] // hl) % 8 == jnp.arange(8)[:, None]
        lm = jnp.where(diag, lens.reshape(g, 2, 8)[:, :, :, None], 0)
        ct = jnp.transpose(cache, (1, 2, 3, 4, 0)).reshape(nr, page, k, b)
        part, lse = pl.pallas_call(
            functools.partial(kernel, n),
            out_shape=(jax.ShapeDtypeStruct((g, 2, 128, lora), jnp.bfloat16), jax.ShapeDtypeStruct((g, 2, 128), jnp.float32)),
            in_specs=[pl.BlockSpec(memory_space=pltpu.VMEM)] * 2 + [pl.BlockSpec(memory_space=pl.ANY)],
            out_specs=(pl.BlockSpec(memory_space=pltpu.VMEM),) * 2,
            scratch_shapes=[
                pltpu.VMEM((3, page, k, b), jnp.bfloat16),
                pltpu.VMEM((nr * page, g, 16, KP), jnp.bfloat16),
                pltpu.VMEM((KP, 256), jnp.bfloat16),
                pltpu.VMEM((2, nr * page, 8, 128), jnp.float32),
                pltpu.SemaphoreType.DMA((3,)),
            ],
            compiler_params=pltpu.CompilerParams(vmem_limit_bytes=67043328),
        )(lm, qa, ct)
        od = lax.all_to_all(part.reshape(g, 2, n, 16, lora), 'dcp', 2, 2, tiled=True)
        le = lax.all_to_all(lse.reshape(g, 2, n, 16), 'dcp', 2, 2, tiled=True)
        top = jnp.max(le, axis=2, keepdims=True)
        w = jnp.exp2(le - top)
        o = jnp.sum(w[..., None] * od.astype(jnp.float32), axis=2) / jnp.sum(w, axis=2)[..., None]
        return o.astype(jnp.bfloat16).reshape(b, hl, lora)

    return jax.shard_map(local, mesh=mesh, in_specs=(P('dp', 'dcp', None), P('dp', None, 'dcp', None, None), P('dp')), out_specs=P('dp', 'dcp', None), check_vma=False)
```

time: 155 us -> 154 us (level)
  Pallas kernels: 0 us -> 61.6 us
  local copies, waits for them, and re-layouts: 61.4 us -> 16.9 us
  matrix products: 33.5 us -> 0 us
  waiting for transfers between devices: 27.6 us -> 51.3 us
  other arithmetic: 7.15 us -> 2.94 us
  starting transfers between devices: 10.1 us -> 7.43 us
    pallas_call x0 -> x1, Pallas kernels: none -> 61.6 us  [local(): pl.pallas_call(functools.partial(kernel, n), out_shape=(jax.ShapeDtypeStr...]
    unnamed x5 -> x3, local copies, waits for them, and re-layouts: 51.3 us -> 2.72 us
    dot_general x2 -> x0, matrix products: 33.5 us -> none  [the longest x1 19.1 us: local(): jnp.einsum('bhk,btk->bht', qa, c, preferred_element_type=jnp.float32)]
    all_gather x1, waiting for transfers between devices: 0.02 us -> 23.9 us  [local(): qa = lax.all_gather(q, 'dcp', axis=0)]
    transpose x0 -> x2, local copies, waits for them, and re-layouts: none -> 6.05 us  [local(): qa = qa.transpose(1, 2, 0, 3, 4, 5).reshape(g, 256, KP)]
    reduce_sum x3 -> x2, other arithmetic: 5.37 us -> 0.53 us  [the longest x1 0.46 us: local(): jnp.sum(w[..., None] * od.astype(jnp.float32), axis=2)]
    all_gather x1 -> x0, local copies, waits for them, and re-layouts: 3.92 us -> none  [local(): qa = lax.all_gather(q, 'dcp', axis=1, tiled=True)]
    all_to_all x2, starting transfers between devices: 10.1 us -> 7.43 us  [the longest x1 3.81 us: local(): lax.all_to_all(part.reshape(g, 2, n, 16, lora), 'dcp', 2, 2, tiled=True)]
  transfers between devices with their start and end apart: 3 -> 3, of which waited for: 1 -> 3; matrix products, arithmetic and copies ran while one was open for 47% -> 4% of each run, Pallas kernels for 0% -> 0%
where the time goes in v1:
time: 154 us
  Pallas kernels  61.6 us (40%)
  waiting for transfers between devices  51.3 us (33%)
  local copies, waits for them, and re-layouts  16.9 us (11%)
  between operations  13.5 us (9%)
  starting transfers between devices  7.43 us (5%)
  other arithmetic  2.94 us (2%)
    pallas_call x1, Pallas kernels, local(): pl.pallas_call(functools.partial(kernel, n), out_shape=(jax.ShapeDtypeStr...  61.6 us
    all_to_all x1, waiting for transfers between devices, local(): lax.all_to_all(part.reshape(g, 2, n, 16, lora), 'dcp', 2, 2, tiled=True)  25.4 us
    all_gather x1, waiting for transfers between devices, local(): qa = lax.all_gather(q, 'dcp', axis=0)  23.9 us
    transpose x2, local copies, waits for them, and re-layouts, local(): qa = qa.transpose(1, 2, 0, 3, 4, 5).reshape(g, 256, KP)  6.05 us
    all_to_all x1, starting transfers between devices, local(): lax.all_to_all(part.reshape(g, 2, n, 16, lora), 'dcp', 2, 2, tiled=True)  3.81 us
    all_to_all x1, starting transfers between devices, local(): le = lax.all_to_all(lse.reshape(g, 2, n, 16), 'dcp', 2, 2, tiled=True)  3.62 us
    reshape x1, local copies, waits for them, and re-layouts, local(): part.reshape(g, 2, n, 16, lora)  3.19 us
  transfers between devices with their start and end apart: 3, of which 3 were waited for; matrix products, arithmetic and copies ran while one was open for 4% of the time, Pallas kernels for 0%

profile of v1, /device:TPU:112, one launch (start us, length us, event | category | flops | bytes accessed | tf_op | source)
XLA Modules:
  0.0 153.7 jit_solution(5558743135462407910)
XLA Ops:
  6.6 1.9 %copy.9 = bf16[128,2,576]{2,0,1:T(8,128)(2,1)} copy(bf16[128,2,576]{0,2,1:T(8,128)(2,1)} %param.3) | data formatting | bytes 589824 | tf_op args[0]
  8.4 0.1 all-gather.3.cloned.1.call-update
  8.5 0.7 broadcast_in_dim.24
  9.2 0.7 broadcast_select_fusion.lm_ref
  10.0 23.9 %all-gather.3.cloned.1.call-done = bf16[1024,2,576]{2,0,1:T(8,128)(2,1)} async-done(((bf16[128,2,576]{2,0,1:T(8,128)(2,1)}), bf16[1024,2,576]{2,0,1:T(8,128)(2,1)}) %all-gather.3.cloned.1.call-update) | async-done | bytes 2359312 | tf_op jit(solution)/shard_map/all_gather | solution.py:108
  33.8 2.0 %pad_bitcast_fusion = bf16[8,2,8,8,2,640]{5,3,1,0,2,4:T(8,128)(2,1)S(1)} fusion(bf16[8,8,2,8,2,576]{5,3,2,1,0,4:T(8,128)(2,1)} %bitcast.18), kind=kLoop, calls=%fused_computation.1 | loop fusion | bytes 4980736 | tf_op jit(solution)/shard_map/transpose | solution.py:110
  35.8 4.0 %copy.10 = bf16[8,2,8,8,2,640]{5,4,3,2,1,0:T(2,128)(2,1)S(1)} copy(bf16[8,2,8,8,2,640]{5,3,1,0,2,4:T(8,128)(2,1)S(1)} %pad_bitcast_fusion) | data formatting | bytes 5242880 | tf_op jit(solution)/shard_map/transpose | solution.py:110
  39.9 2.5 %reshape.78.q_ref = bf16[8,256,640]{2,1,0:T(8,128)(2,1)} reshape(bf16[8,2,8,8,2,640]{5,4,3,2,1,0:T(2,128)(2,1)S(1)} %copy.10) | data formatting | bytes 5242880 | tf_op jit(solution)/shard_map/reshape | solution.py:110
  42.3 61.6 %shard_map.37 = (bf16[8,2,128,512]{3,2,1,0:T(8,128)(2,1)}, f32[8,2,128]{2,1,0:T(2,128)}) custom-call(s32[8,2,8,128]{3,2,1,0:T(8,128)} %broadcast_select_fusion.lm_ref, bf16[8,256,640]{2,1,0:T(8,128)(2,1)} %reshape.78.q_ref, bf16[32,8,576,128]{3,2,1,0:T(8,128)(2,1)} %bitcast.17), custom_call_target="tpu_custom_call" | custom-call | tf_op jit(solution)/shard_map/pallas_call | solution.py:115
  104.0 0.8 reshape.80
  104.8 0.7 reshape.84
  105.5 3.6 %all-to-all-start = ((f32[8,1,256]{2,1,0:T(1,128)}), f32[8,1,256]{2,1,0:T(1,128)S(1)}, u32[]{:S(2)}, u32[]{:S(2)}) async-start(f32[8,1,256]{2,1,0:T(1,128)} %reshape.84), calls=%async_computation | async-start | bytes 16384 | tf_op jit(solution)/shard_map/all_to_all | solution.py:130
  109.1 3.2 %copy.13 = bf16[8,2,8,16,512]{4,3,1,0,2:T(8,128)(2,1)} copy(bf16[8,2,8,16,512]{4,3,2,1,0:T(8,128)(2,1)} %bitcast.19) | data formatting | bytes 4194304 | tf_op jit(solution)/shard_map/reshape | solution.py:129
  112.3 1.9 %all-to-all-done = f32[8,1,256]{2,1,0:T(1,128)S(1)} async-done(((f32[8,1,256]{2,1,0:T(1,128)}), f32[8,1,256]{2,1,0:T(1,128)S(1)}, u32[]{:S(2)}, u32[]{:S(2)}) %all-to-all-start) | async-done | bytes 8224 | tf_op jit(solution)/shard_map/all_to_all | solution.py:130
  114.3 3.8 %all-to-all-start.1 = ((bf16[8,2,8,16,512]{4,3,1,0,2:T(8,128)(2,1)}), bf16[8,2,8,16,512]{4,3,1,0,2:T(8,128)(2,1)S(1)}, u32[]{:S(2)}, u32[]{:S(2)}) async-start(bf16[8,2,8,16,512]{4,3,1,0,2:T(8,128)(2,1)} %copy.13), calls=%async_computation.1 | async-start | bytes 4194304 | tf_op jit(solution)/shard_map/all_to_all | solution.py:129
  118.1 0.5 broadcast.68
  118.6 0.7 reduce
  119.3 0.1 reshape.85
  119.4 0.1 fusion.1
  119.5 0.1 div.18
  119.6 25.4 %all-to-all-done.1 = bf16[8,2,8,16,512]{4,3,1,0,2:T(8,128)(2,1)S(1)} async-done(((bf16[8,2,8,16,512]{4,3,1,0,2:T(8,128)(2,1)}), bf16[8,2,8,16,512]{4,3,1,0,2:T(8,128)(2,1)S(1)}, u32[]{:S(2)}, u32[]{:S(2)}) %all-to-all-start.1) | async-done | bytes 2097184 | tf_op jit(solution)/shard_map/all_to_all | solution.py:129
  145.0 0.5 multiply_reduce_fusion
  145.5 0.3 reduce_sum.21
  145.8 1.0 divide_convert_fusion
  (5 shorter events, 0.1 us)
Async XLA Ops:
  6.5 27.3 %all-gather.3.cloned.1.call-start = ((), (), s32[]{:S(2)}) async-start(), calls=%async_computation.2 | async-start | bytes 2949120 | tf_op jit(solution)/shard_map/all_gather | solution.py:108
  105.5 8.7 %all-to-all-start = ((f32[8,1,256]{2,1,0:T(1,128)}), f32[8,1,256]{2,1,0:T(1,128)S(1)}, u32[]{:S(2)}, u32[]{:S(2)}) async-start(f32[8,1,256]{2,1,0:T(1,128)} %reshape.84), calls=%async_computation | async-start | bytes 16384 | tf_op jit(solution)/shard_map/all_to_all | solution.py:130
  114.3 30.8 %all-to-all-start.1 = ((bf16[8,2,8,16,512]{4,3,1,0,2:T(8,128)(2,1)}), bf16[8,2,8,16,512]{4,3,1,0,2:T(8,128)(2,1)S(1)}, u32[]{:S(2)}, u32[]{:S(2)}) async-start(bf16[8,2,8,16,512]{4,3,1,0,2:T(8,128)(2,1)} %copy.13), calls=%async_computation.1 | async-start | bytes 4194304 | tf_op jit(solution)/shard_map/all_to_all | solution.py:129
Sparse Core Ops, SparseCore 0:
  8.9 24.8 all-gather.2

commit v2 on v0

v2 whole, which is shorter than its diff:
```python
import functools
import jax
import jax.numpy as jnp
from jax import lax
from jax.experimental import pallas as pl
from jax.experimental.pallas import tpu as pltpu
from jax.sharding import PartitionSpec as P

ROPE = 64
QK_DIM = 192
SCALE = QK_DIM ** -0.5
LOG2E = 1.4426950408889634
KP = 640
TQ = 64
TV = 64
MESH = pl.DeviceIdType.MESH


def kernel(lm_ref, q_ref, c_hbm, o_ref, y, qall, qt, s0_ref, s1_ref, accs, arecv, part, precv, lses, lrecv, cols,
           csem, qs, qr, ss, sr, ps, pr, ls, lr):
    me = lax.axis_index('dcp')
    dp = lax.axis_index('dp')
    x, c = me // 2, lax.rem(me, 2)
    nx = 4
    n = 2 * nx
    nr, page, k, b = c_hbm.shape
    g = b // 16
    t = nr * page
    lora = k - ROPE

    def at(dx, same):
        xx = lax.rem(x + dx + nx, nx)
        return (dp, xx * 2 + (c if same else 1 - c))

    def slot(dx):
        return c * nx + lax.rem(x + dx + nx, nx)

    def pslot(dx):
        return (1 - c) * nx + lax.rem(x + dx + nx, nx)

    def fetch(r):
        return pltpu.make_async_copy(c_hbm.at[r], y.at[pl.ds(r * page, page), 0:k], csem.at[r])

    for r in range(nr):
        fetch(r).start()

    barrier = pltpu.get_barrier_semaphore()
    for dev in (at(1, True), at(-1, True), at(2, True), at(0, False)):
        pl.semaphore_signal(barrier, inc=1, device_id=dev, device_id_type=MESH)
    pl.semaphore_wait(barrier, 4)

    def rc(src, dst, s, r, dev):
        return pltpu.make_async_remote_copy(src_ref=src, dst_ref=dst, send_sem=s, recv_sem=r, device_id=dev, device_id_type=MESH)

    def qsend(gi, kind):
        sl = {0: slot(0), 1: slot(0), 2: slot(0), 3: slot(-1), 4: slot(-1), 5: slot(1), 6: slot(1), 7: slot(2)}[kind]
        dev = {0: at(1, True), 1: at(-1, True), 4: at(1, True), 6: at(-1, True)}.get(kind, at(0, False))
        half = {4: 0, 6: 1}.get(kind)
        if kind <= 2:
            src, dst = q_ref.at[gi], qall.at[gi, sl]
        elif half is None:
            src = dst = qall.at[gi, sl]
        else:
            src = dst = qall.at[gi, sl, half]
        return rc(src, dst, qs.at[gi, kind], qr.at[gi, kind], dev)

    def qwait(gi, kind):
        sl = {0: slot(-1), 1: slot(1), 2: pslot(0), 3: pslot(-1), 4: slot(2), 5: pslot(1), 6: slot(2), 7: pslot(2)}[kind]
        half = {4: 0, 6: 1}.get(kind)
        ref = qall.at[gi, sl] if half is None else qall.at[gi, sl, half]
        rc(ref, ref, qs.at[gi, kind], qr.at[gi, kind], at(0, False)).wait_recv()

    for gi in range(g):
        for kind in range(3):
            qsend(gi, kind).start()
        qall[gi, slot(0)] = q_ref[gi]

    def relay1(gi):
        qwait(gi, 0)
        qsend(gi, 4).start()
        qsend(gi, 3).start()
        qwait(gi, 1)
        qsend(gi, 6).start()
        qsend(gi, 5).start()

    def relay2(gi):
        qwait(gi, 4)
        qwait(gi, 6)
        qsend(gi, 7).start()

    def load(r, _):
        fetch(r).wait()
        for p in range(page):
            i = r * page + p
            for kt in range(lora // 128):
                y[i, kt * 128:(kt + 1) * 128] = y[i, kt * 128:(kt + 1) * 128].T
            xr = y[i, lora:k]
            y[i, lora:KP] = jnp.concatenate([xr, jnp.zeros((KP - k, b), xr.dtype)], 0).T
        return 0

    def seg(i, _):
        lax.fori_loop(i * (nr // g), (i + 1) * (nr // g), load, 0)

        @pl.when(i >= 1)
        def _():
            relay1(i - 1)

        @pl.when(i >= 3)
        def _():
            relay2(i - 3)
        return 0

    lax.fori_loop(0, g, seg, 0)
    relay1(g - 1)
    for i in range(g - 3, g):
        relay2(i)

    def rows(ti, tn, gi, nk):
        parts = [y[pl.ds(ti, tn), pl.ds(kt * 128 + gi * 16, 16)].reshape(tn * 16, 128) for kt in range(nk)]
        return jnp.concatenate(parts, axis=1)

    def loadq(gi):
        for kind in (2, 3, 5, 7):
            qwait(gi, kind)
        q0 = qall[gi, :, 0].reshape(128, KP)
        q1 = qall[gi, :, 1].reshape(128, KP)
        qt[...] = jnp.concatenate([q0, q1], axis=0).T

    def qk(gi, j, s_ref, m):
        s = jnp.dot(rows(j * TQ, TQ, gi, KP // 128), qt[...], preferred_element_type=jnp.float32)
        s = s.reshape(TQ, 2, 8, 256)
        ti = lax.broadcasted_iota(jnp.int32, (TQ, 1, 1), 0) + j * TQ
        pos = ((ti // page) * n + me) * page + lax.rem(ti, page)
        out = []
        for o in range(2):
            so = s[:, o, :, o * 128:(o + 1) * 128] * (SCALE * LOG2E)
            so = jnp.where(pos < lm_ref[gi, o][None], so, -jnp.inf)
            s_ref[o, pl.ds(j * TQ, TQ)] = so
            out.append(jnp.maximum(m[o], jnp.max(so, axis=0)))
        return tuple(out)

    def fin(m):
        return tuple(jnp.max(a, axis=0, keepdims=True) for a in m)

    def fix(m):
        return jnp.where(m == -jnp.inf, 0.0, m)

    lane = lax.broadcasted_iota(jnp.int32, (128, TV * 16), 1)
    first = lax.rem(lane, 16) < 8

    def pv(gi, j, s_ref, mf, l, acc):
        pe = []
        lo = []
        for o in range(2):
            p = jnp.exp2(s_ref[o, pl.ds(j * TV, TV)] - mf[o][None])
            lo.append(l[o] + jnp.sum(p, axis=0))
            pe.append(p)
        pm = jnp.concatenate(pe, axis=1).astype(jnp.bfloat16).reshape(TV * 16, 128).T
        z = jnp.zeros_like(pm)
        pt = jnp.concatenate([jnp.where(first, pm, z), jnp.where(first, z, pm)], axis=0)
        acc = acc + jnp.dot(pt, rows(j * TV, TV, gi, lora // 128), preferred_element_type=jnp.float32)
        return tuple(lo), acc

    def asend(gi):
        return rc(accs.at[gi, 1 - c], arecv.at[gi], ss.at[gi], sr.at[gi], at(0, False))

    def put(gi, m, l, acc):
        for o in range(2):
            lo = jnp.sum(l[o], axis=0, keepdims=True)
            st = jnp.concatenate([m[o], lo, jnp.zeros((6, 128), jnp.float32)], axis=0)
            for h in range(2):
                r0 = o * 128 + h * 64
                accs[gi, h, o, 0:64] = acc[r0:r0 + 64]
                accs[gi, h, o, 64:72, 0:128] = st
        asend(gi).start()

    def psend(gi, dx):
        return rc(part.at[gi, lax.rem(x + dx, nx)], precv.at[gi, 3 - dx], ps.at[gi, dx - 1], pr.at[gi, 3 - dx], at(dx, True))

    def lsend(gi, dx):
        return rc(lses.at[gi], lrecv.at[gi, 3 - dx], ls.at[gi, dx - 1], lr.at[gi, 3 - dx], at(dx, True))

    def merge(gi):
        asend(gi).wait_recv()
        for o in range(2):
            m1, l1 = accs[gi, c, o, 64:65, 0:128], accs[gi, c, o, 65:66, 0:128]
            m2, l2 = arecv[gi, o, 64:65, 0:128], arecv[gi, o, 65:66, 0:128]
            mm = jnp.maximum(m1, m2)
            ms = fix(mm)
            w1, w2 = jnp.exp2(m1 - ms), jnp.exp2(m2 - ms)
            lt = w1 * l1 + w2 * l2
            has = lt > 0.0
            lsafe = jnp.where(has, lt, 1.0)
            lses[gi, o:o + 1] = jnp.where(has, ms + jnp.log2(lsafe), -jnp.inf)
            wr = jnp.concatenate([w1 / lsafe, w2 / lsafe, jnp.zeros((6, 128), jnp.float32)], axis=0)
            cols[...] = wr.T
            w = cols[pl.ds(c * 64, 64)]
            od = accs[gi, c, o, 0:64] * w[:, 0:1] + arecv[gi, o, 0:64] * w[:, 1:2]
            part[gi, :, o] = od.astype(jnp.bfloat16).reshape(nx, 16, lora)
        for dx in (2, 1, 3):
            psend(gi, dx).start()
            lsend(gi, dx).start()

    def final(gi):
        for dx in range(1, 4):
            psend(gi, dx).wait_recv()
            lsend(gi, dx).wait_recv()
        for o in range(2):
            le = [lses[gi, o:o + 1]] + [lrecv[gi, i, o:o + 1] for i in range(3)]
            top = functools.reduce(jnp.maximum, le)
            w = [jnp.exp2(a - top) for a in le]
            tot = sum(w)
            wr = jnp.concatenate([a / tot for a in w] + [jnp.zeros((4, 128), jnp.float32)], axis=0)
            cols[...] = wr.T
            wc = cols[pl.ds(c * 64 + x * 16, 16)]
            od = part[gi, x, o].astype(jnp.float32) * wc[:, 0:1]
            for i in range(3):
                od = od + precv[gi, i, o].astype(jnp.float32) * wc[:, i + 1:i + 2]
            o_ref[gi, o] = od.astype(jnp.bfloat16)

    m0 = (jnp.full((8, 128), -jnp.inf, jnp.float32),) * 2
    l0 = (jnp.zeros((8, 128), jnp.float32),) * 2
    a0 = jnp.zeros((256, lora), jnp.float32)

    def after(ga):
        @pl.when(ga >= 1)
        def _():
            merge(ga - 1)

        @pl.when(ga >= 3)
        def _():
            final(ga - 3)

    def both(ga, sa, gb, sb, m):
        loadq(gb)
        mf = [fix(a) for a in m]
        mn, l, acc = m0, l0, a0
        for j in range(t // TQ):
            mn = qk(gb, j, sb, mn)
            l, acc = pv(ga, j, sa, mf, l, acc)
        put(ga, m, l, acc)
        after(ga)
        return fin(mn)

    def only_qk(gi, s_ref):
        loadq(gi)
        m = m0
        for j in range(t // TQ):
            m = qk(gi, j, s_ref, m)
        return fin(m)

    def only_pv(gi, s_ref, m):
        mf = [fix(a) for a in m]
        l, acc = l0, a0
        for j in range(t // TV):
            l, acc = pv(gi, j, s_ref, mf, l, acc)
        put(gi, m, l, acc)
        after(gi)

    def pair(i, m):
        m = both(2 * i, s0_ref, 2 * i + 1, s1_ref, m)
        return both(2 * i + 1, s1_ref, 2 * i + 2, s0_ref, m)

    m = only_qk(0, s0_ref)
    m = lax.fori_loop(0, g // 2 - 1, pair, m)
    m = both(g - 2, s0_ref, g - 1, s1_ref, m)
    only_pv(g - 1, s1_ref, m)
    merge(g - 1)
    for gi in range(g - 3, g):
        final(gi)

    def drain(gi, _):
        for kind in range(8):
            qsend(gi, kind).wait_send()
        asend(gi).wait_send()
        for dx in range(1, 4):
            psend(gi, dx).wait_send()
            lsend(gi, dx).wait_send()
        return 0

    lax.fori_loop(0, g, drain, 0)


def solution(mesh):
    n = mesh.shape['dcp']
    nx = n // 2

    def local(q, cache, lens):
        b, hl, k = q.shape
        nr, page = cache.shape[1], cache.shape[3]
        lora = k - ROPE
        g = b // 16
        t = nr * page
        qo = jnp.pad(q.reshape(g, 2, 16, k), [(0, 0)] * 3 + [(0, KP - k)])
        lane = jnp.arange(128)
        diag = (lane[None, :] // hl) % 8 == jnp.arange(8)[:, None]
        lm = jnp.where(diag, lens.reshape(g, 2, 8)[:, :, :, None], 0)
        ct = jnp.transpose(cache, (1, 2, 3, 4, 0)).reshape(nr, page, k, b)
        o = pl.pallas_call(
            kernel,
            out_shape=jax.ShapeDtypeStruct((g, 2, 16, lora), jnp.bfloat16),
            in_specs=[pl.BlockSpec(memory_space=pltpu.VMEM)] * 2 + [pl.BlockSpec(memory_space=pl.ANY)],
            out_specs=pl.BlockSpec(memory_space=pltpu.VMEM),
            scratch_shapes=[
                pltpu.VMEM((t, KP, b), jnp.bfloat16),
                pltpu.VMEM((g, n, 2, 16, KP), jnp.bfloat16),
                pltpu.VMEM((KP, 256), jnp.bfloat16),
                pltpu.VMEM((2, t, 8, 128), jnp.float32),
                pltpu.VMEM((2, t, 8, 128), jnp.float32),
                pltpu.VMEM((g, 2, 2, 72, lora), jnp.float32),
                pltpu.VMEM((g, 2, 72, lora), jnp.float32),
                pltpu.VMEM((g, nx, 2, 16, lora), jnp.bfloat16),
                pltpu.VMEM((g, nx - 1, 2, 16, lora), jnp.bfloat16),
                pltpu.VMEM((g, 2, 128), jnp.float32),
                pltpu.VMEM((g, nx - 1, 2, 128), jnp.float32),
                pltpu.VMEM((128, 8), jnp.float32),
                pltpu.SemaphoreType.DMA((nr,)),
                pltpu.SemaphoreType.DMA((g, 8)),
                pltpu.SemaphoreType.DMA((g, 8)),
                pltpu.SemaphoreType.DMA((g,)),
                pltpu.SemaphoreType.DMA((g,)),
                pltpu.SemaphoreType.DMA((g, nx - 1)),
                pltpu.SemaphoreType.DMA((g, nx - 1)),
                pltpu.SemaphoreType.DMA((g, nx - 1)),
                pltpu.SemaphoreType.DMA((g, nx - 1)),
            ],
            compiler_params=pltpu.CompilerParams(vmem_limit_bytes=67043328, collective_id=0, has_side_effects=True),
        )(lm, qo, ct)
        return o.reshape(b, hl, lora)

    return jax.shard_map(local, mesh=mesh, in_specs=(P('dp', 'dcp', None), P('dp', None, 'dcp', None, None), P('dp')), out_specs=P('dp', 'dcp', None), check_vma=False)
```

time: 155 us -> 67.6 us (0.44)
  Pallas kernels: 0 us -> 61.5 us
  local copies, waits for them, and re-layouts: 61.4 us -> 4.91 us
  matrix products: 33.5 us -> 0 us
  waiting for transfers between devices: 27.6 us -> 0 us
  between operations: 13.5 us -> 0.04 us
  starting transfers between devices: 10.1 us -> 0 us
  other arithmetic: 7.15 us -> 0.73 us
    pallas_call x0 -> x1, Pallas kernels: none -> 61.5 us  [local(): pl.pallas_call(kernel, out_shape=jax.ShapeDtypeStruct((g, 2, 16, lora), j...]
    unnamed x5 -> x1, local copies, waits for them, and re-layouts: 51.3 us -> 1.42 us
    dot_general x2 -> x0, matrix products: 33.5 us -> none  [the longest x1 19.1 us: local(): jnp.einsum('bhk,btk->bht', qa, c, preferred_element_type=jnp.float32)]
    all_to_all x2 -> x0, waiting for transfers between devices: 26.8 us -> none  [the longest x1 26.8 us: local(): od = lax.all_to_all(od.reshape(b, n, hl, lorav), 'dcp', 1, 1, tiled=True)]
    all_to_all x2 -> x0, starting transfers between devices: 10.1 us -> none  [the longest x1 5.3 us: local(): lse = lax.all_to_all(lse.reshape(b, n, hl), 'dcp', 1, 1, tiled=True)]
    reduce_sum x3 -> x0, other arithmetic: 5.37 us -> none  [the longest x1 2.76 us: local(): jnp.sum(w[:, :, :, None] * od.astype(jnp.float32), axis=1)]
    all_gather x1 -> x0, local copies, waits for them, and re-layouts: 3.92 us -> none  [local(): qa = lax.all_gather(q, 'dcp', axis=1, tiled=True)]
    reshape x2, local copies, waits for them, and re-layouts: 5.72 us -> 2 us  [the longest x1 1.75 us: local(): return o.reshape(b, hl, lora)]
  transfers between devices with their start and end apart: 3 -> 0, of which waited for: 1 -> 0; matrix products, arithmetic and copies ran while one was open for 47% -> 0% of each run, Pallas kernels for 0% -> 0%
where the time goes in v2:
time: 67.6 us; the launch traced here: 67.2 us
  Pallas kernels  61.5 us (91%)
  local copies, waits for them, and re-layouts  4.91 us (7%)
  other arithmetic  0.73 us (1%)
    pallas_call x1, Pallas kernels, local(): pl.pallas_call(kernel, out_shape=jax.ShapeDtypeStruct((g, 2, 16, lora), j...  61.5 us
    reshape x1, local copies, waits for them, and re-layouts, local(): return o.reshape(b, hl, lora)  1.75 us
    unnamed x1, local copies, waits for them, and re-layouts  1.42 us

profile of v2, /device:TPU:112, one launch (start us, length us, event | category | flops | bytes accessed | tf_op | source)
XLA Modules:
  0.0 67.2 jit_solution(11789291121477737263)
XLA Ops:
  0.0 1.4 %copy.6 = bf16[128,2,576]{2,1,0:T(2,128)(2,1)S(1)} copy(bf16[128,2,576]{0,2,1:T(8,128)(2,1)} %param.3) | data formatting | bytes 589824 | tf_op args[0]
  1.4 0.2 reshape.64
  1.7 0.7 %pad.4.q_ref = bf16[8,2,16,640]{3,2,1,0:T(8,128)(2,1)} pad(bf16[8,2,16,576]{3,2,1,0:T(8,128)(2,1)S(1)} %reshape.64, bf16[]{:T(256)} %constant.32.clone.1), padding=0_0x0_0x0_0x0_64 | pad | bytes 622594 | tf_op jit(solution)/shard_map/jit(_pad)/pad | solution.py:294
  2.4 0.7 %broadcast_in_dim.21 = s32[8,2,8]{2,1,0:T(2,128)S(1)} reshape(s32[128]{0:T(128)} %param.5) | data formatting | bytes 1024 | tf_op jit(solution)/shard_map/jit(_where)/broadcast_in_dim | solution.py:297
  3.2 0.7 %broadcast_select_fusion.lm_ref = s32[8,2,8,128]{3,2,1,0:T(8,128)} fusion(s32[8,2,8]{2,1,0:T(2,128)S(1)} %broadcast_in_dim.21, pred[8,128]{1,0:T(8,128)(4,1)S(1)} %iota_compare_fusion), kind=kLoop, calls=%fused_computation | loop fusion | flops 16384 | bytes 67072 | tf_op jit(solution)/shard_map/jit(_where)/select_n | solution.py:297
  3.9 61.5 %shard_map.37 = bf16[8,2,16,512]{3,2,1,0:T(8,128)(2,1)} custom-call(s32[8,2,8,128]{3,2,1,0:T(8,128)} %broadcast_select_fusion.lm_ref, bf16[8,2,16,640]{3,2,1,0:T(8,128)(2,1)} %pad.4.q_ref, bf16[32,8,576,128]{3,2,1,0:T(8,128)(2,1)} %bitcast.7), custom_call_target="tpu_custom_call" | custom-call | tf_op jit(solution)/shard_map/pallas_call | solution.py:299
  65.4 1.8 %reshape.66 = bf16[128,2,512]{2,1,0:T(2,128)(2,1)} reshape(bf16[8,2,16,512]{3,2,1,0:T(8,128)(2,1)} %shard_map.37) | data formatting | bytes 524288 | tf_op jit(solution)/shard_map/reshape | solution.py:329
  (2 shorter events, 0.0 us)

commit v3 on v2

--- a/solution.py
+++ b/solution.py
@@ -16,7 +16,7 @@
 MESH = pl.DeviceIdType.MESH
 
 
-def kernel(lm_ref, q_ref, c_hbm, o_ref, y, qall, qt, s0_ref, s1_ref, accs, arecv, part, precv, lses, lrecv, cols,
+def kernel(lens_ref, qn_ref, c_hbm, o_ref, y, q_ref, lm_ref, qall, qt, s0_ref, s1_ref, accs, arecv, part, precv, lses, lrecv, cols,
            csem, qs, qr, ss, sr, ps, pr, ls, lr):
     me = lax.axis_index('dcp')
     dp = lax.axis_index('dp')
@@ -27,6 +27,8 @@
     g = b // 16
     t = nr * page
     lora = k - ROPE
+    bf = jnp.bfloat16
+    f32 = jnp.float32
 
     def at(dx, same):
         xx = lax.rem(x + dx + nx, nx)
@@ -47,6 +49,26 @@
     barrier = pltpu.get_barrier_semaphore()
     for dev in (at(1, True), at(-1, True), at(2, True), at(0, False)):
         pl.semaphore_signal(barrier, inc=1, device_id=dev, device_id_type=MESH)
+
+    for kt in range(KP // 128):
+        r0, r1 = kt * 128, min(kt * 128 + 128, k)
+        hs = []
+        for h in range(2):
+            xq = qn_ref[h, r0:r1]
+            if r1 - r0 < 128:
+                xq = jnp.concatenate([xq, jnp.zeros((128 - (r1 - r0), b), bf)], 0)
+            hs.append(xq.T.astype(f32).reshape(g, 2, 1, 8, 128))
+        q_ref[:, :, :, r0:r0 + 128] = jnp.concatenate(hs, axis=2).reshape(g, 2, 16, 128).astype(bf)
+
+    sub = lax.broadcasted_iota(jnp.int32, (8, 128), 0)
+    diag = lax.rem(lax.broadcasted_iota(jnp.int32, (8, 128), 1), 8) == sub
+    for gi in range(g):
+        for o in range(2):
+            v = jnp.zeros((8, 128), jnp.int32)
+            for i in range(8):
+                v = jnp.where(sub == i, lens_ref[gi * 16 + o * 8 + i], v)
+            lm_ref[gi, o] = jnp.where(diag, v, 0)
+
     pl.semaphore_wait(barrier, 4)
 
     def rc(src, dst, s, r, dev):
@@ -98,22 +120,16 @@
             y[i, lora:KP] = jnp.concatenate([xr, jnp.zeros((KP - k, b), xr.dtype)], 0).T
         return 0
 
-    def seg(i, _):
-        lax.fori_loop(i * (nr // g), (i + 1) * (nr // g), load, 0)
-
-        @pl.when(i >= 1)
-        def _():
-            relay1(i - 1)
-
-        @pl.when(i >= 3)
-        def _():
-            relay2(i - 3)
+    def step(r, _):
+        load(r, 0)
+        u = r - 6
+        for j, f in ((u, relay1), (u - 7, relay2)):
+            @pl.when((j >= 0) & (lax.rem(j + 30, 3) == 0) & (j < 3 * g))
+            def _():
+                f(j // 3)
         return 0
 
-    lax.fori_loop(0, g, seg, 0)
-    relay1(g - 1)
-    for i in range(g - 3, g):
-        relay2(i)
+    lax.fori_loop(0, nr, step, 0)
 
     def rows(ti, tn, gi, nk):
         parts = [y[pl.ds(ti, tn), pl.ds(kt * 128 + gi * 16, 16)].reshape(tn * 16, 128) for kt in range(nk)]
@@ -180,8 +196,10 @@
     def lsend(gi, dx):
         return rc(lses.at[gi], lrecv.at[gi, 3 - dx], ls.at[gi, dx - 1], lr.at[gi, 3 - dx], at(dx, True))
 
+    def merge_wait(gi):
+        asend(gi).wait_recv()
+
     def merge(gi):
-        asend(gi).wait_recv()
         for o in range(2):
             m1, l1 = accs[gi, c, o, 64:65, 0:128], accs[gi, c, o, 65:66, 0:128]
             m2, l2 = arecv[gi, o, 64:65, 0:128], arecv[gi, o, 65:66, 0:128]
@@ -192,54 +210,71 @@
             has = lt > 0.0
             lsafe = jnp.where(has, lt, 1.0)
             lses[gi, o:o + 1] = jnp.where(has, ms + jnp.log2(lsafe), -jnp.inf)
-            wr = jnp.concatenate([w1 / lsafe, w2 / lsafe, jnp.zeros((6, 128), jnp.float32)], axis=0)
-            cols[...] = wr.T
-            w = cols[pl.ds(c * 64, 64)]
+            wr = jnp.concatenate([w1 / lsafe, w2 / lsafe, jnp.zeros((6, 128), f32)], axis=0)
+            cols[o] = wr.T
+            w = cols[o, pl.ds(c * 64, 64)]
             od = accs[gi, c, o, 0:64] * w[:, 0:1] + arecv[gi, o, 0:64] * w[:, 1:2]
-            part[gi, :, o] = od.astype(jnp.bfloat16).reshape(nx, 16, lora)
+            part[gi, :, o] = od.astype(bf).reshape(nx, 16, lora)
+
+    def merge_send(gi):
         for dx in (2, 1, 3):
             psend(gi, dx).start()
             lsend(gi, dx).start()
 
-    def final(gi):
+    def final_wait(gi):
         for dx in range(1, 4):
             psend(gi, dx).wait_recv()
             lsend(gi, dx).wait_recv()
+
+    def final(gi):
         for o in range(2):
             le = [lses[gi, o:o + 1]] + [lrecv[gi, i, o:o + 1] for i in range(3)]
             top = functools.reduce(jnp.maximum, le)
             w = [jnp.exp2(a - top) for a in le]
             tot = sum(w)
-            wr = jnp.concatenate([a / tot for a in w] + [jnp.zeros((4, 128), jnp.float32)], axis=0)
-            cols[...] = wr.T
-            wc = cols[pl.ds(c * 64 + x * 16, 16)]
-            od = part[gi, x, o].astype(jnp.float32) * wc[:, 0:1]
+            wr = jnp.concatenate([a / tot for a in w] + [jnp.zeros((4, 128), f32)], axis=0)
+            cols[2 + o] = wr.T
+            wc = cols[2 + o, pl.ds(c * 64 + x * 16, 16)]
+            od = part[gi, x, o].astype(f32) * wc[:, 0:1]
             for i in range(3):
-                od = od + precv[gi, i, o].astype(jnp.float32) * wc[:, i + 1:i + 2]
-            o_ref[gi, o] = od.astype(jnp.bfloat16)
+                od = od + precv[gi, i, o].astype(f32) * wc[:, i + 1:i + 2]
+            o_ref[gi, o] = od.astype(bf)
 
     m0 = (jnp.full((8, 128), -jnp.inf, jnp.float32),) * 2
     l0 = (jnp.zeros((8, 128), jnp.float32),) * 2
     a0 = jnp.zeros((256, lora), jnp.float32)
 
-    def after(ga):
+    LAG = 4
+
+    def top(ga):
         @pl.when(ga >= 1)
         def _():
-            merge(ga - 1)
-
-        @pl.when(ga >= 3)
+            merge_wait(ga - 1)
+
+        @pl.when(ga >= LAG)
         def _():
-            final(ga - 3)
+            final_wait(ga - LAG)
+
+    def mid(ga):
+        merge(lax.select(ga >= 1, ga - 1, g))
+        final(lax.select(ga >= LAG, ga - LAG, g))
+
+    def end(ga, m, l, acc):
+        @pl.when(ga >= 1)
+        def _():
+            merge_send(ga - 1)
+        put(ga, m, l, acc)
 
     def both(ga, sa, gb, sb, m):
+        top(ga)
         loadq(gb)
+        mid(ga)
         mf = [fix(a) for a in m]
         mn, l, acc = m0, l0, a0
         for j in range(t // TQ):
             mn = qk(gb, j, sb, mn)
             l, acc = pv(ga, j, sa, mf, l, acc)
-        put(ga, m, l, acc)
-        after(ga)
+        end(ga, m, l, acc)
         return fin(mn)
 
     def only_qk(gi, s_ref):
@@ -250,23 +285,33 @@
         return fin(m)
 
     def only_pv(gi, s_ref, m):
+        top(gi)
+        mid(gi)
         mf = [fix(a) for a in m]
         l, acc = l0, a0
         for j in range(t // TV):
             l, acc = pv(gi, j, s_ref, mf, l, acc)
-        put(gi, m, l, acc)
-        after(gi)
+        end(gi, m, l, acc)
 
     def pair(i, m):
         m = both(2 * i, s0_ref, 2 * i + 1, s1_ref, m)
         return both(2 * i + 1, s1_ref, 2 * i + 2, s0_ref, m)
 
     m = only_qk(0, s0_ref)
+    for i in range((nr - 13 + 2) // 3, g):
+        relay2(i)
     m = lax.fori_loop(0, g // 2 - 1, pair, m)
-    m = both(g - 2, s0_ref, g - 1, s1_ref, m)
-    only_pv(g - 1, s1_ref, m)
+    last = jnp.int32(g - 1)
+    m = both(last - 1, s0_ref, last, s1_ref, m)
+    only_pv(last, s1_ref, m)
+    for gi in range(g - LAG, g - 2):
+        final_wait(gi)
+        final(gi)
+    merge_wait(g - 1)
     merge(g - 1)
-    for gi in range(g - 3, g):
+    merge_send(g - 1)
+    for gi in range(g - 2, g):
+        final_wait(gi)
         final(gi)
 
     def drain(gi, _):
@@ -291,29 +336,28 @@
         lora = k - ROPE
         g = b // 16
         t = nr * page
-        qo = jnp.pad(q.reshape(g, 2, 16, k), [(0, 0)] * 3 + [(0, KP - k)])
-        lane = jnp.arange(128)
-        diag = (lane[None, :] // hl) % 8 == jnp.arange(8)[:, None]
-        lm = jnp.where(diag, lens.reshape(g, 2, 8)[:, :, :, None], 0)
+        qn = jnp.transpose(q, (1, 2, 0))
         ct = jnp.transpose(cache, (1, 2, 3, 4, 0)).reshape(nr, page, k, b)
         o = pl.pallas_call(
             kernel,
-            out_shape=jax.ShapeDtypeStruct((g, 2, 16, lora), jnp.bfloat16),
-            in_specs=[pl.BlockSpec(memory_space=pltpu.VMEM)] * 2 + [pl.BlockSpec(memory_space=pl.ANY)],
+            out_shape=jax.ShapeDtypeStruct((g + 1, 2, 16, lora), jnp.bfloat16),
+            in_specs=[pl.BlockSpec(memory_space=pltpu.SMEM), pl.BlockSpec(memory_space=pltpu.VMEM), pl.BlockSpec(memory_space=pl.ANY)],
             out_specs=pl.BlockSpec(memory_space=pltpu.VMEM),
             scratch_shapes=[
                 pltpu.VMEM((t, KP, b), jnp.bfloat16),
+                pltpu.VMEM((g, 2, 16, KP), jnp.bfloat16),
+                pltpu.VMEM((g, 2, 8, 128), jnp.int32),
                 pltpu.VMEM((g, n, 2, 16, KP), jnp.bfloat16),
                 pltpu.VMEM((KP, 256), jnp.bfloat16),
                 pltpu.VMEM((2, t, 8, 128), jnp.float32),
                 pltpu.VMEM((2, t, 8, 128), jnp.float32),
-                pltpu.VMEM((g, 2, 2, 72, lora), jnp.float32),
-                pltpu.VMEM((g, 2, 72, lora), jnp.float32),
-                pltpu.VMEM((g, nx, 2, 16, lora), jnp.bfloat16),
-                pltpu.VMEM((g, nx - 1, 2, 16, lora), jnp.bfloat16),
-                pltpu.VMEM((g, 2, 128), jnp.float32),
-                pltpu.VMEM((g, nx - 1, 2, 128), jnp.float32),
-                pltpu.VMEM((128, 8), jnp.float32),
+                pltpu.VMEM((g + 1, 2, 2, 72, lora), jnp.float32),
+                pltpu.VMEM((g + 1, 2, 72, lora), jnp.float32),
+                pltpu.VMEM((g + 1, nx, 2, 16, lora), jnp.bfloat16),
+                pltpu.VMEM((g + 1, nx - 1, 2, 16, lora), jnp.bfloat16),
+                pltpu.VMEM((g + 1, 2, 128), jnp.float32),
+                pltpu.VMEM((g + 1, nx - 1, 2, 128), jnp.float32),
+                pltpu.VMEM((4, 128, 8), jnp.float32),
                 pltpu.SemaphoreType.DMA((nr,)),
                 pltpu.SemaphoreType.DMA((g, 8)),
                 pltpu.SemaphoreType.DMA((g, 8)),
@@ -325,7 +369,7 @@
                 pltpu.SemaphoreType.DMA((g, nx - 1)),
             ],
             compiler_params=pltpu.CompilerParams(vmem_limit_bytes=67043328, collective_id=0, has_side_effects=True),
-        )(lm, qo, ct)
-        return o.reshape(b, hl, lora)
+        )(lens, qn, ct)
+        return o[:g].reshape(g, 2, hl, 8, lora).transpose(0, 1, 3, 2, 4).reshape(b, hl, lora)
 
     return jax.shard_map(local, mesh=mesh, in_specs=(P('dp', 'dcp', None), P('dp', None, 'dcp', None, None), P('dp')), out_specs=P('dp', 'dcp', None), check_vma=False)

time: 67.6 us -> 70.1 us (1.037)
  Pallas kernels: 61.5 us -> 68.1 us
  local copies, waits for them, and re-layouts: 4.91 us -> 1.91 us
  other arithmetic: 0.73 us -> 0 us
    pallas_call x1, Pallas kernels: 61.5 us -> 68.1 us  [local(): pl.pallas_call(kernel, out_shape=jax.ShapeDtypeStruct((g + 1, 2, 16, lora...]
    reshape x2 -> x0, local copies, waits for them, and re-layouts: 2 us -> none  [the longest x1 1.75 us: local(): return o.reshape(b, hl, lora)]
    transpose x0 -> x2, local copies, waits for them, and re-layouts: none -> 1.91 us  [local(): o[:g].reshape(g, 2, hl, 8, lora).transpose(0, 1, 3, 2, 4)]
    unnamed x1 -> x0, local copies, waits for them, and re-layouts: 1.42 us -> none
    pad x1 -> x0, local copies, waits for them, and re-layouts: 0.74 us -> none  [local(): qo = jnp.pad(q.reshape(g, 2, 16, k), [(0, 0)] * 3 + [(0, KP - k)])]
    broadcast_in_dim x1 -> x0, local copies, waits for them, and re-layouts: 0.74 us -> none  [local(): lm = jnp.where(diag, lens.reshape(g, 2, 8)[:, :, :, None], 0)]
    select_n x2 -> x0, other arithmetic: 0.72 us -> none  [the longest x1 0.71 us: local(): lm = jnp.where(diag, lens.reshape(g, 2, 8)[:, :, :, None], 0)]
where the time goes in v3:
time: 70.1 us; the launch traced here: 70 us
  Pallas kernels  68.1 us (97%)
  local copies, waits for them, and re-layouts  1.91 us (3%)
    pallas_call x1, Pallas kernels, local(): pl.pallas_call(kernel, out_shape=jax.ShapeDtypeStruct((g + 1, 2, 16, lora...  68.1 us
    transpose x2, local copies, waits for them, and re-layouts, local(): o[:g].reshape(g, 2, hl, 8, lora).transpose(0, 1, 3, 2, 4)  1.91 us

profile of v3, /device:TPU:112, one launch (start us, length us, event | category | flops | bytes accessed | tf_op | source)
XLA Modules:
  0.0 70.0 jit_solution(9519925181081644524)
XLA Ops:
  0.0 68.1 %shard_map.37 = bf16[9,2,16,512]{3,2,1,0:T(8,128)(2,1)} custom-call(s32[128]{0:T(128)} %lens_ref.1, bf16[2,576,128]{2,1,0:T(8,128)(2,1)} %bitcast.12, bf16[32,8,576,128]{3,2,1,0:T(8,128)(2,1)} %bitcast.11), custom_call_target="tpu_custom_call" | custom-call | tf_op jit(solution)/shard_map/pallas_call | solution.py:341
  68.1 1.0 %slice_bitcast_fusion = bf16[8,2,8,2,512]{4,2,3,1,0:T(8,128)(2,1)S(1)} fusion(bf16[9,2,16,512]{3,2,1,0:T(8,128)(2,1)} %shard_map.37), kind=kLoop, calls=%fused_computation | loop fusion | bytes 524288 | tf_op jit(solution)/shard_map/transpose | solution.py:373
  69.1 0.9 %copy.5 = bf16[8,2,8,2,512]{4,3,2,1,0:T(2,128)(2,1)} copy(bf16[8,2,8,2,512]{4,2,3,1,0:T(8,128)(2,1)S(1)} %slice_bitcast_fusion) | data formatting | bytes 524288 | tf_op jit(solution)/shard_map/transpose | solution.py:373

commit v4 on v3

v4 whole, which is shorter than its diff:
```python
import functools
import jax
import jax.numpy as jnp
from jax import lax
from jax.experimental import pallas as pl
from jax.experimental.pallas import tpu as pltpu
from jax.sharding import PartitionSpec as P

ROPE = 64
QK_DIM = 192
SCALE = QK_DIM ** -0.5
LOG2E = 1.4426950408889634
KP = 640
TQ = 64
TV = 64
NS = 4
NU = 4
MESH = pl.DeviceIdType.MESH


def kernel(lens_ref, qn_ref, c_hbm, o_ref, ylo, yhi, q_ref, lm_ref, qall, qt, s0_ref, s1_ref, accs, arecv, part, precv, lses, lrecv, cols,
           csem, qs, qr, ss, sr, ps, pr, ls, lr):
    me = lax.axis_index('dcp')
    dp = lax.axis_index('dp')
    x, c = me // 2, lax.rem(me, 2)
    nx = 4
    n = 2 * nx
    nr, page, k, b = c_hbm.shape
    g = b // 16
    t = nr * page
    lora = k - ROPE
    bf = jnp.bfloat16
    f32 = jnp.float32

    def at(dx, same):
        xx = lax.rem(x + dx + nx, nx)
        return (dp, xx * 2 + (c if same else 1 - c))

    def slot(dx):
        return c * nx + lax.rem(x + dx + nx, nx)

    def pslot(dx):
        return (1 - c) * nx + lax.rem(x + dx + nx, nx)

    def fetch(r, y):
        return pltpu.make_async_copy(c_hbm.at[r], y.at[pl.ds(lax.rem(r, nr // 2) * page, page), 0:k], csem.at[r])

    for r in range(nr):
        fetch(r, ylo if r < nr // 2 else yhi).start()

    barrier = pltpu.get_barrier_semaphore()
    for dev in (at(1, True), at(-1, True), at(2, True), at(0, False)):
        pl.semaphore_signal(barrier, inc=1, device_id=dev, device_id_type=MESH)

    for kt in range(KP // 128):
        r0, r1 = kt * 128, min(kt * 128 + 128, k)
        hs = []
        for h in range(2):
            xq = qn_ref[h, r0:r1]
            if r1 - r0 < 128:
                xq = jnp.concatenate([xq, jnp.zeros((128 - (r1 - r0), b), bf)], 0)
            hs.append(xq.T.astype(f32).reshape(g, 2, 1, 8, 128))
        q_ref[:, :, :, r0:r0 + 128] = jnp.concatenate(hs, axis=2).reshape(g, 2, 16, 128).astype(bf)

    sub = lax.broadcasted_iota(jnp.int32, (8, 128), 0)
    lane8 = lax.rem(lax.broadcasted_iota(jnp.int32, (8, 128), 1), 8)
    diag = lane8 == sub
    turn = lax.rem(sub - lane8 + 8, 8)
    for gi in range(g):
        for o in range(2):
            v = jnp.zeros((8, 128), jnp.int32)
            for i in range(8):
                v = jnp.where(lane8 == i, lens_ref[gi * 16 + o * 8 + i], v)
            lm_ref[gi, o] = v

    def load(r, y):
        for i in range(2):
            fetch(2 * r + i, y).wait()
        for p in range(2 * page):
            i = lax.rem(r, nr // 4) * 2 * page + p
            for kt in range(lora // 128):
                y[i, kt * 128:(kt + 1) * 128] = y[i, kt * 128:(kt + 1) * 128].T
            xr = y[i, lora:k]
            y[i, lora:KP] = jnp.concatenate([xr, jnp.zeros((KP - k, b), xr.dtype)], 0).T

    load(0, ylo)
    pl.semaphore_wait(barrier, 4)

    def rc(src, dst, s, r, dev):
        return pltpu.make_async_remote_copy(src_ref=src, dst_ref=dst, send_sem=s, recv_sem=r, device_id=dev, device_id_type=MESH)

    def qsend(gi, kind):
        sl = {0: slot(0), 1: slot(0), 2: slot(0), 3: slot(-1), 4: slot(-1), 5: slot(1), 6: slot(1), 7: slot(2)}[kind]
        dev = {0: at(1, True), 1: at(-1, True), 4: at(1, True), 6: at(-1, True)}.get(kind, at(0, False))
        half = {4: 0, 6: 1}.get(kind)
        if kind <= 2:
            src, dst = q_ref.at[gi], qall.at[gi, sl]
        elif half is None:
            src = dst = qall.at[gi, sl]
        else:
            src = dst = qall.at[gi, sl, half]
        return rc(src, dst, qs.at[gi, kind], qr.at[gi, kind], dev)

    def qwait(gi, kind):
        sl = {0: slot(-1), 1: slot(1), 2: pslot(0), 3: pslot(-1), 4: slot(2), 5: pslot(1), 6: slot(2), 7: pslot(2)}[kind]
        half = {4: 0, 6: 1}.get(kind)
        ref = qall.at[gi, sl] if half is None else qall.at[gi, sl, half]
        rc(ref, ref, qs.at[gi, kind], qr.at[gi, kind], at(0, False)).wait_recv()

    AHEAD = 3

    def own(gi):
        for kind in range(3):
            qsend(gi, kind).start()

    for gi in range(AHEAD):
        own(gi)
    for gi in range(g):
        qall[gi, slot(0)] = q_ref[gi]

    def relay1(gi):
        qwait(gi, 0)
        qsend(gi, 4).start()
        qsend(gi, 3).start()
        qwait(gi, 1)
        qsend(gi, 6).start()
        qsend(gi, 5).start()

        @pl.when(gi + AHEAD < g)
        def _():
            own(gi + AHEAD)

    def relay2(gi):
        qwait(gi, 4)
        qwait(gi, 6)
        qsend(gi, 7).start()

    R1, R2 = 4, 8

    def relays(r):
        for rr, f in ((R1, relay1), (R2, relay2)):
            j = r - rr

            @pl.when((j >= 0) & (lax.rem(j + 30, 3) == 0) & (2 * (j // 3) < g))
            def _():
                f(2 * (j // 3))

            @pl.when((j >= 2) & (lax.rem(j + 28, 3) == 0) & (2 * ((j - 2) // 3) + 1 < g))
            def _():
                f(2 * ((j - 2) // 3) + 1)

    def count(rr):
        return len([gi for gi in range(g) if rr + (3 * gi + 1) // 2 < nr // 2])

    n1, n2 = count(R1), count(R2)

    def rows(ti, tn, gi, nk):
        y = ylo if ti < t // 2 else yhi
        ti = ti % (t // 2)
        parts = [y[pl.ds(ti, tn), pl.ds(kt * 128 + gi * 16, 16)].reshape(tn * 16, 128) for kt in range(nk)]
        return jnp.concatenate(parts, axis=1)

    def loadq(gi):
        for kind in (2, 3, 5, 7):
            qwait(gi, kind)
        reload(gi)

    def reload(gi):
        q0 = qall[gi, :, 0].reshape(128, KP)
        q1 = qall[gi, :, 1].reshape(128, KP)
        qt[...] = jnp.concatenate([q0, q1], axis=0).T

    def qk(gi, j, s_ref):
        s = jnp.dot(rows(j * TQ, TQ, gi, KP // 128), qt[...], preferred_element_type=jnp.float32)
        s = s.reshape(TQ // 8, 8, 2, 8, 256)
        blk = lax.broadcasted_iota(jnp.int32, (TQ // 8, 1, 1), 0) + j * (TQ // 8)
        pos = (blk * n + me) * page + turn[None]
        for o in range(2):
            d = s[:, 0, o, :, o * 128:(o + 1) * 128]
            for i in range(1, 8):
                d = jnp.where((turn == i)[None], pltpu.roll(s[:, i, o, :, o * 128:(o + 1) * 128], i, 1), d)
            d = jnp.where(pos < lm_ref[gi, o][None], d * (SCALE * LOG2E), -jnp.inf)
            s_ref[gi // 2, o, pl.ds(j * (TQ // 8), TQ // 8)] = d

    def qks(gi, j0, j1, s_ref):
        for j in range(j0, j1):
            qk(gi, j, s_ref)

    def fix(m):
        return jnp.where(m == -jnp.inf, 0.0, m)

    def maxes(gi, s_ref):
        return [jnp.max(jnp.max(s_ref[gi // 2, o], axis=0), axis=0, keepdims=True) for o in range(2)]

    lane = lax.broadcasted_iota(jnp.int32, (128, TV * 16), 1)
    first = lax.rem(lane, 16) < 8

    def pv(gi, j, s_ref, mf, l, acc):
        pe = []
        lo = []
        for o in range(2):
            p = jnp.exp2(s_ref[gi // 2, o, pl.ds(j * (TV // 8), TV // 8)] - mf[o][None])
            lo.append(l[o] + jnp.sum(p, axis=0))
            q = [p] + [pltpu.roll(p, 8 - i, 1) for i in range(1, 8)]
            q = jnp.stack([jnp.where(diag[None], a, 0.0) for a in q], axis=1)
            pe.append(q.reshape(TV, 8, 128))
        pm = jnp.concatenate(pe, axis=1).astype(bf).reshape(TV * 16, 128).T
        z = jnp.zeros_like(pm)
        pt = jnp.concatenate([jnp.where(first, pm, z), jnp.where(first, z, pm)], axis=0)
        acc = acc + jnp.dot(pt, rows(j * TV, TV, gi, lora // 128), preferred_element_type=jnp.float32)
        return tuple(lo), acc

    def asend(gi):
        return rc(accs.at[lax.rem(gi, NS), 1 - c], arecv.at[lax.rem(gi, NS)], ss.at[gi], sr.at[gi], at(0, False))

    def put(gi, m, l, acc):
        gs = lax.rem(gi, NS)

        @pl.when(gi >= NS)
        def _():
            asend(gi - NS).wait_send()

        for o in range(2):
            lo = jnp.sum(l[o], axis=0, keepdims=True)
            st = jnp.concatenate([m[o], lo, jnp.zeros((6, 128), jnp.float32)], axis=0)
            for h in range(2):
                r0 = o * 128 + h * 64
                accs[gs, h, o, 0:64] = acc[r0:r0 + 64]
                accs[gs, h, o, 64:72, 0:128] = st
        asend(gi).start()

    def psend(gi, dx):
        return rc(part.at[gi, lax.rem(x + dx, nx)], precv.at[gi, 3 - dx], ps.at[gi, dx - 1], pr.at[gi, 3 - dx], at(dx, True))

    def lsend(gi, dx):
        return rc(lses.at[gi], lrecv.at[gi, 3 - dx], ls.at[gi, dx - 1], lr.at[gi, 3 - dx], at(dx, True))

    def merge_wait(gi):
        asend(gi).wait_recv()

    def merge(gi, live=None):
        gs = lax.rem(gi, NS)
        if live is not None:
            gs, gi = lax.select(live, gs, NS), lax.select(live, gi, g)
        for o in range(2):
            m1, l1 = accs[gs, c, o, 64:65, 0:128], accs[gs, c, o, 65:66, 0:128]
            m2, l2 = arecv[gs, o, 64:65, 0:128], arecv[gs, o, 65:66, 0:128]
            mm = jnp.maximum(m1, m2)
            ms = fix(mm)
            w1, w2 = jnp.exp2(m1 - ms), jnp.exp2(m2 - ms)
            lt = w1 * l1 + w2 * l2
            has = lt > 0.0
            lsafe = jnp.where(has, lt, 1.0)
            lses[gi, o:o + 1] = jnp.where(has, ms + jnp.log2(lsafe), -jnp.inf)
            wr = jnp.concatenate([w1 / lsafe, w2 / lsafe, jnp.zeros((6, 128), f32)], axis=0)
            cols[o] = wr.T
            w = cols[o, pl.ds(c * 64, 64)]
            od = accs[gs, c, o, 0:64] * w[:, 0:1] + arecv[gs, o, 0:64] * w[:, 1:2]
            part[gi, :, o] = od.astype(bf).reshape(nx, 16, lora)

    def merge_send(gi):
        for dx in (2, 1, 3):
            psend(gi, dx).start()
            lsend(gi, dx).start()

    def final_wait(gi):
        for dx in range(1, 4):
            psend(gi, dx).wait_recv()
            lsend(gi, dx).wait_recv()

    def final(gi, live=None):
        og = gi
        if live is not None:
            og, gi = lax.select(live, gi, 0), lax.select(live, gi, g)
        for o in range(2):
            le = [lses[gi, o:o + 1]] + [lrecv[gi, i, o:o + 1] for i in range(3)]
            top = functools.reduce(jnp.maximum, le)
            w = [jnp.exp2(a - top) for a in le]
            tot = sum(w)
            wr = jnp.concatenate([a / tot for a in w] + [jnp.zeros((4, 128), f32)], axis=0)
            cols[2 + o] = wr.T
            wc = cols[2 + o, pl.ds(c * 64 + x * 16, 16)]
            od = part[gi, x, o].astype(f32) * wc[:, 0:1]
            for i in range(3):
                od = od + precv[gi, i, o].astype(f32) * wc[:, i + 1:i + 2]
            o_ref[pl.ds(og * 16 + o * 8, 8)] = jnp.stack([od[0:8], od[8:16]], axis=1).astype(bf)

    l0 = (jnp.zeros((8, 128), jnp.float32),) * 2
    a0 = jnp.zeros((256, lora), jnp.float32)

    LAG = 5
    ML = 2

    def top(ga):
        @pl.when(ga + n1 < g)
        def _():
            relay1(ga + n1)

        @pl.when(ga + n2 < g)
        def _():
            relay2(ga + n2)

        @pl.when(ga >= ML)
        def _():
            merge_wait(ga - ML)

        @pl.when(ga >= LAG)
        def _():
            final_wait(ga - LAG)

    def mid(ga):
        merge(lax.rem(ga - ML + NS * g, NS * g), ga >= ML)
        final(ga - LAG, ga >= LAG)

    def end(ga, m, l, acc):
        @pl.when(ga >= ML)
        def _():
            merge_send(ga - ML)
        put(ga, m, l, acc)

    NJ = t // TQ

    def both(ga, sa, gb, sb, j0):
        top(ga)
        (reload if j0 else loadq)(gb)
        mid(ga)
        m = maxes(ga, sa)
        mf = [fix(a) for a in m]
        l, acc = l0, a0
        done = j0
        for j in range(NJ):
            todo = j0 + (NJ - j0) * (j + 1) // NJ
            qks(gb, done, todo, sb)
            done = todo
            l, acc = pv(ga, j, sa, mf, l, acc)
        end(ga, m, l, acc)

    def only_pv(gi, s_ref):
        top(gi)
        mid(gi)
        m = maxes(gi, s_ref)
        mf = [fix(a) for a in m]
        l, acc = l0, a0
        for j in range(NJ):
            l, acc = pv(gi, j, s_ref, mf, l, acc)
        end(gi, m, l, acc)

    def pair(i, _, j0):
        both(2 * i, s0_ref, 2 * i + 1, s1_ref, j0)
        both(2 * i + 1, s1_ref, 2 * i + 2, s0_ref, j0)
        return 0

    H = NJ // 2
    U0 = nr // 2 - NU

    def astep(r, _, y):
        relays(r)
        load(r, y)
        return 0

    def bstep(i, _):
        for s_ref, e in ((s0_ref, 0), (s1_ref, 1)):
            r = U0 + 2 * i + e
            relays(r)
            loadq(2 * i + e)
            load(r, yhi)
            qks(2 * i + e, 0, H, s_ref)
        return 0

    lax.fori_loop(1, nr // 4, functools.partial(astep, y=ylo), 0)
    lax.fori_loop(nr // 4, U0, functools.partial(astep, y=yhi), 0)
    lax.fori_loop(0, NU // 2, bstep, 0)
    reload(0)
    qks(0, H, NJ, s0_ref)
    lax.fori_loop(0, NU // 2 - 1, functools.partial(pair, j0=H), 0)
    both(jnp.int32(NU - 2), s0_ref, jnp.int32(NU - 1), s1_ref, H)
    both(jnp.int32(NU - 1), s1_ref, jnp.int32(NU), s0_ref, 0)
    lax.fori_loop(NU // 2, g // 2 - 1, functools.partial(pair, j0=0), 0)
    last = jnp.int32(g - 1)
    both(last - 1, s0_ref, last, s1_ref, 0)
    only_pv(last, s1_ref)
    for gi in range(g - ML, g - 1):
        merge_wait(gi)
        merge(gi)
        merge_send(gi)
    for gi in range(g - LAG, g - ML - 1):
        final_wait(gi)
        final(gi)
    merge_wait(g - 1)
    merge(g - 1)
    merge_send(g - 1)
    def drain(gi, _):
        for kind in range(8):
            qsend(gi, kind).wait_send()
        @pl.when(gi >= g - NS)
        def _():
            asend(gi).wait_send()

        for dx in range(1, 4):
            psend(gi, dx).wait_send()
            lsend(gi, dx).wait_send()
        return 0

    lax.fori_loop(0, g, drain, 0)

    for gi in range(g - ML - 1, g):
        final_wait(gi)
        final(gi)


def solution(mesh):
    n = mesh.shape['dcp']
    nx = n // 2

    def local(q, cache, lens):
        b, hl, k = q.shape
        nr, page = cache.shape[1], cache.shape[3]
        lora = k - ROPE
        g = b // 16
        t = nr * page
        qn = jnp.transpose(q, (1, 2, 0))
        ct = jnp.transpose(cache, (1, 2, 3, 4, 0)).reshape(nr, page, k, b)
        o = pl.pallas_call(
            kernel,
            out_shape=jax.ShapeDtypeStruct((b, hl, lora), jnp.bfloat16),
            in_specs=[pl.BlockSpec(memory_space=pltpu.SMEM), pl.BlockSpec(memory_space=pltpu.VMEM), pl.BlockSpec(memory_space=pl.ANY)],
            out_specs=pl.BlockSpec(memory_space=pltpu.VMEM),
            scratch_shapes=[
                pltpu.VMEM((t // 2, KP, b), jnp.bfloat16),
                pltpu.VMEM((t // 2, KP, b), jnp.bfloat16),
                pltpu.VMEM((g, 2, 16, KP), jnp.bfloat16),
                pltpu.VMEM((g, 2, 8, 128), jnp.int32),
                pltpu.VMEM((g, n, 2, 16, KP), jnp.bfloat16),
                pltpu.VMEM((KP, 256), jnp.bfloat16),
                pltpu.VMEM((g // 2, 2, t // 8, 8, 128), jnp.float32),
                pltpu.VMEM((g // 2, 2, t // 8, 8, 128), jnp.float32),
                pltpu.VMEM((NS + 1, 2, 2, 72, lora), jnp.float32),
                pltpu.VMEM((NS + 1, 2, 72, lora), jnp.float32),
                pltpu.VMEM((g + 1, nx, 2, 16, lora), jnp.bfloat16),
                pltpu.VMEM((g + 1, nx - 1, 2, 16, lora), jnp.bfloat16),
                pltpu.VMEM((g + 1, 2, 128), jnp.float32),
                pltpu.VMEM((g + 1, nx - 1, 2, 128), jnp.float32),
                pltpu.VMEM((4, 128, 8), jnp.float32),
                pltpu.SemaphoreType.DMA((nr,)),
                pltpu.SemaphoreType.DMA((g, 8)),
                pltpu.SemaphoreType.DMA((g, 8)),
                pltpu.SemaphoreType.DMA((g,)),
                pltpu.SemaphoreType.DMA((g,)),
                pltpu.SemaphoreType.DMA((g, nx - 1)),
                pltpu.SemaphoreType.DMA((g, nx - 1)),
                pltpu.SemaphoreType.DMA((g, nx - 1)),
                pltpu.SemaphoreType.DMA((g, nx - 1)),
            ],
            compiler_params=pltpu.CompilerParams(vmem_limit_bytes=67043328, collective_id=0, has_side_effects=True),
        )(lens, qn, ct)
        return o

    return jax.shard_map(local, mesh=mesh, in_specs=(P('dp', 'dcp', None), P('dp', None, 'dcp', None, None), P('dp')), out_specs=P('dp', 'dcp', None), check_vma=False)
```

time: 70.1 us -> 57.7 us (0.82)
  Pallas kernels: 68.1 us -> 55.7 us
    pallas_call x1, Pallas kernels: 68.1 us -> 55.7 us  [local(): pl.pallas_call(kernel, out_shape=jax.ShapeDtypeStruct((b, hl, lora), jnp....]
    transpose x2 -> x0, local copies, waits for them, and re-layouts: 1.91 us -> none  [local(): o[:g].reshape(g, 2, hl, 8, lora).transpose(0, 1, 3, 2, 4)]
    unnamed x0 -> x1, local copies, waits for them, and re-layouts: none -> 1.83 us
where the time goes in v4:
time: 57.7 us; the launch traced here: 57.6 us
  Pallas kernels  55.7 us (97%)
  local copies, waits for them, and re-layouts  1.83 us (3%)
    pallas_call x1, Pallas kernels, local(): pl.pallas_call(kernel, out_shape=jax.ShapeDtypeStruct((b, hl, lora), jnp....  55.7 us
    unnamed x1, local copies, waits for them, and re-layouts  1.83 us

profile of v4, /device:TPU:112, one launch (start us, length us, event | category | flops | bytes accessed | tf_op | source)
XLA Modules:
  0.0 57.6 jit_solution(14410731680845099100)
XLA Ops:
  0.0 55.7 %shard_map.37 = bf16[128,2,512]{2,1,0:T(2,128)(2,1)} custom-call(s32[128]{0:T(128)} %lens_ref.1, bf16[2,576,128]{2,1,0:T(8,128)(2,1)} %bitcast.7, bf16[32,8,576,128]{3,2,1,0:T(8,128)(2,1)} %bitcast.6), custom_call_target="tpu_custom_call" | custom-call | tf_op jit(solution)/shard_map/pallas_call | solution.py:423
  55.7 1.8 %copy.6 = bf16[128,2,512]{2,1,0:T(2,128)(2,1)} copy(bf16[128,2,512]{2,1,0:T(2,128)(2,1)} %shard_map.37) | data formatting | bytes 524288

commit v5 on v4

--- a/solution.py
+++ b/solution.py
@@ -18,8 +18,8 @@
 MESH = pl.DeviceIdType.MESH
 
 
-def kernel(lens_ref, qn_ref, c_hbm, o_ref, ylo, yhi, q_ref, lm_ref, qall, qt, s0_ref, s1_ref, accs, arecv, part, precv, lses, lrecv, cols,
-           csem, qs, qr, ss, sr, ps, pr, ls, lr):
+def kernel(lens_hbm, qn_hbm, c_hbm, o_hbm, lens_ref, qn_ref, o_ref, ylo, yhi, q_ref, lm_ref, qall, qt, s0_ref, s1_ref, accs, arecv, part, precv, lses, lrecv, cols,
+           isem, osem, csem, qs, qr, ss, sr, ps, pr, ls, lr):
     me = lax.axis_index('dcp')
     dp = lax.axis_index('dp')
     x, c = me // 2, lax.rem(me, 2)
@@ -39,19 +39,21 @@
     def slot(dx):
         return c * nx + lax.rem(x + dx + nx, nx)
 
-    def pslot(dx):
-        return (1 - c) * nx + lax.rem(x + dx + nx, nx)
-
     def fetch(r, y):
         return pltpu.make_async_copy(c_hbm.at[r], y.at[pl.ds(lax.rem(r, nr // 2) * page, page), 0:k], csem.at[r])
 
-    for r in range(nr):
-        fetch(r, ylo if r < nr // 2 else yhi).start()
+    qin = pltpu.make_async_copy(qn_hbm, qn_ref, isem.at[0])
+    lin = pltpu.make_async_copy(lens_hbm, lens_ref, isem.at[1])
+    qin.start()
+    lin.start()
+    for r in range(4):
+        fetch(r, ylo).start()
 
     barrier = pltpu.get_barrier_semaphore()
     for dev in (at(1, True), at(-1, True), at(2, True), at(0, False)):
         pl.semaphore_signal(barrier, inc=1, device_id=dev, device_id_type=MESH)
 
+    qin.wait()
     for kt in range(KP // 128):
         r0, r1 = kt * 128, min(kt * 128 + 128, k)
         hs = []
@@ -66,6 +68,9 @@
     lane8 = lax.rem(lax.broadcasted_iota(jnp.int32, (8, 128), 1), 8)
     diag = lane8 == sub
     turn = lax.rem(sub - lane8 + 8, 8)
+    lin.wait()
+    for r in range(4, nr):
+        fetch(r, ylo if r < nr // 2 else yhi).start()
     for gi in range(g):
         for o in range(2):
             v = jnp.zeros((8, 128), jnp.int32)
@@ -90,27 +95,28 @@
         return pltpu.make_async_remote_copy(src_ref=src, dst_ref=dst, send_sem=s, recv_sem=r, device_id=dev, device_id_type=MESH)
 
     def qsend(gi, kind):
-        sl = {0: slot(0), 1: slot(0), 2: slot(0), 3: slot(-1), 4: slot(-1), 5: slot(1), 6: slot(1), 7: slot(2)}[kind]
-        dev = {0: at(1, True), 1: at(-1, True), 4: at(1, True), 6: at(-1, True)}.get(kind, at(0, False))
-        half = {4: 0, 6: 1}.get(kind)
-        if kind <= 2:
-            src, dst = q_ref.at[gi], qall.at[gi, sl]
-        elif half is None:
-            src = dst = qall.at[gi, sl]
+        dev = {0: at(1, True), 1: at(-1, True), 2: at(1, True), 3: at(-1, True), 4: at(0, False)}[kind]
+        if kind <= 1:
+            src, dst = q_ref.at[gi], qall.at[gi, slot(0)]
+        elif kind <= 3:
+            src = dst = qall.at[gi, slot(-1 if kind == 2 else 1), kind - 2]
         else:
-            src = dst = qall.at[gi, sl, half]
+            src = dst = qall.at[gi, pl.ds(c * nx, nx)]
         return rc(src, dst, qs.at[gi, kind], qr.at[gi, kind], dev)
 
     def qwait(gi, kind):
-        sl = {0: slot(-1), 1: slot(1), 2: pslot(0), 3: pslot(-1), 4: slot(2), 5: pslot(1), 6: slot(2), 7: pslot(2)}[kind]
-        half = {4: 0, 6: 1}.get(kind)
-        ref = qall.at[gi, sl] if half is None else qall.at[gi, sl, half]
+        if kind <= 1:
+            ref = qall.at[gi, slot(-1 if kind == 0 else 1)]
+        elif kind <= 3:
+            ref = qall.at[gi, slot(2), kind - 2]
+        else:
+            ref = qall.at[gi, pl.ds((1 - c) * nx, nx)]
         rc(ref, ref, qs.at[gi, kind], qr.at[gi, kind], at(0, False)).wait_recv()
 
     AHEAD = 3
 
     def own(gi):
-        for kind in range(3):
+        for kind in range(2):
             qsend(gi, kind).start()
 
     for gi in range(AHEAD):
@@ -120,20 +126,18 @@
 
     def relay1(gi):
         qwait(gi, 0)
+        qsend(gi, 2).start()
+        qwait(gi, 1)
+        qsend(gi, 3).start()
+
+        @pl.when(gi + AHEAD < g)
+        def _():
+            own(gi + AHEAD)
+
+    def relay2(gi):
+        qwait(gi, 2)
+        qwait(gi, 3)
         qsend(gi, 4).start()
-        qsend(gi, 3).start()
-        qwait(gi, 1)
-        qsend(gi, 6).start()
-        qsend(gi, 5).start()
-
-        @pl.when(gi + AHEAD < g)
-        def _():
-            own(gi + AHEAD)
-
-    def relay2(gi):
-        qwait(gi, 4)
-        qwait(gi, 6)
-        qsend(gi, 7).start()
 
     R1, R2 = 4, 8
 
@@ -161,8 +165,7 @@
         return jnp.concatenate(parts, axis=1)
 
     def loadq(gi):
-        for kind in (2, 3, 5, 7):
-            qwait(gi, kind)
+        qwait(gi, 4)
         reload(gi)
 
     def reload(gi):
@@ -268,6 +271,10 @@
             psend(gi, dx).wait_recv()
             lsend(gi, dx).wait_recv()
 
+    def oput(gi):
+        w = pl.ds(gi * 16, 16)
+        return pltpu.make_async_copy(o_ref.at[w], o_hbm.at[w], osem.at[gi])
+
     def final(gi, live=None):
         og = gi
         if live is not None:
@@ -316,6 +323,11 @@
         @pl.when(ga >= ML)
         def _():
             merge_send(ga - ML)
+
+        @pl.when(ga >= LAG)
+        def _():
+            oput(ga - LAG).start()
+
         put(ga, m, l, acc)
 
     NJ = t // TQ
@@ -386,11 +398,12 @@
     for gi in range(g - LAG, g - ML - 1):
         final_wait(gi)
         final(gi)
+        oput(gi).start()
     merge_wait(g - 1)
     merge(g - 1)
     merge_send(g - 1)
     def drain(gi, _):
-        for kind in range(8):
+        for kind in range(5):
             qsend(gi, kind).wait_send()
         @pl.when(gi >= g - NS)
         def _():
@@ -406,6 +419,9 @@
     for gi in range(g - ML - 1, g):
         final_wait(gi)
         final(gi)
+        oput(gi).start()
+    for gi in range(g):
+        oput(gi).wait()
 
 
 def solution(mesh):
@@ -423,9 +439,12 @@
         o = pl.pallas_call(
             kernel,
             out_shape=jax.ShapeDtypeStruct((b, hl, lora), jnp.bfloat16),
-            in_specs=[pl.BlockSpec(memory_space=pltpu.SMEM), pl.BlockSpec(memory_space=pltpu.VMEM), pl.BlockSpec(memory_space=pl.ANY)],
-            out_specs=pl.BlockSpec(memory_space=pltpu.VMEM),
+            in_specs=[pl.BlockSpec(memory_space=pl.ANY)] * 3,
+            out_specs=pl.BlockSpec(memory_space=pl.ANY),
             scratch_shapes=[
+                pltpu.SMEM((b,), jnp.int32),
+                pltpu.VMEM((hl, k, b), jnp.bfloat16),
+                pltpu.VMEM((b, hl, lora), jnp.bfloat16),
                 pltpu.VMEM((t // 2, KP, b), jnp.bfloat16),
                 pltpu.VMEM((t // 2, KP, b), jnp.bfloat16),
                 pltpu.VMEM((g, 2, 16, KP), jnp.bfloat16),
@@ -441,9 +460,11 @@
                 pltpu.VMEM((g + 1, 2, 128), jnp.float32),
                 pltpu.VMEM((g + 1, nx - 1, 2, 128), jnp.float32),
                 pltpu.VMEM((4, 128, 8), jnp.float32),
+                pltpu.SemaphoreType.DMA((2,)),
+                pltpu.SemaphoreType.DMA((g,)),
                 pltpu.SemaphoreType.DMA((nr,)),
-                pltpu.SemaphoreType.DMA((g, 8)),
-                pltpu.SemaphoreType.DMA((g, 8)),
+                pltpu.SemaphoreType.DMA((g, 5)),
+                pltpu.SemaphoreType.DMA((g, 5)),
                 pltpu.SemaphoreType.DMA((g,)),
                 pltpu.SemaphoreType.DMA((g,)),
                 pltpu.SemaphoreType.DMA((g, nx - 1)),

time: 57.7 us -> 56.4 us (0.977)
  Pallas kernels: 55.7 us -> 54.4 us
    pallas_call x1, Pallas kernels: 55.7 us -> 54.4 us  [local(): pl.pallas_call(kernel, out_shape=jax.ShapeDtypeStruct((b, hl, lora), jnp....]
where the time goes in v5:
time: 56.4 us; the launch traced here: 56.3 us
  Pallas kernels  54.4 us (96%)
  local copies, waits for them, and re-layouts  1.83 us (3%)
    pallas_call x1, Pallas kernels, local(): pl.pallas_call(kernel, out_shape=jax.ShapeDtypeStruct((b, hl, lora), jnp....  54.4 us
    unnamed x1, local copies, waits for them, and re-layouts  1.83 us

profile of v5, /device:TPU:112, one launch (start us, length us, event | category | flops | bytes accessed | tf_op | source)
XLA Modules:
  0.0 56.3 jit_solution(4705860265696626019)
XLA Ops:
  0.0 54.4 %shard_map.37 = bf16[128,2,512]{2,1,0:T(2,128)(2,1)} custom-call(s32[128]{0:T(128)} %lens_hbm.1, bf16[2,576,128]{2,1,0:T(8,128)(2,1)} %bitcast.7, bf16[32,8,576,128]{3,2,1,0:T(8,128)(2,1)} %bitcast.6), custom_call_target="tpu_custom_call" | custom-call | tf_op jit(solution)/shard_map/pallas_call | solution.py:439
  54.4 1.8 %copy.6 = bf16[128,2,512]{2,1,0:T(2,128)(2,1)} copy(bf16[128,2,512]{2,1,0:T(2,128)(2,1)} %shard_map.37) | data formatting | bytes 524288

commit v6 on v5

--- a/solution.py
+++ b/solution.py
@@ -113,7 +113,7 @@
             ref = qall.at[gi, pl.ds((1 - c) * nx, nx)]
         rc(ref, ref, qs.at[gi, kind], qr.at[gi, kind], at(0, False)).wait_recv()
 
-    AHEAD = 3
+    AHEAD = 4
 
     def own(gi):
         for kind in range(2):
@@ -350,12 +350,18 @@
     def only_pv(gi, s_ref):
         top(gi)
         mid(gi)
+        merge_send(gi - ML)
+        oput(gi - LAG).start()
         m = maxes(gi, s_ref)
         mf = [fix(a) for a in m]
         l, acc = l0, a0
         for j in range(NJ):
+            if j == NJ // 2:
+                merge_wait(gi - 1)
+                merge(gi - 1)
+                merge_send(gi - 1)
             l, acc = pv(gi, j, s_ref, mf, l, acc)
-        end(gi, m, l, acc)
+        put(gi, m, l, acc)
 
     def pair(i, _, j0):
         both(2 * i, s0_ref, 2 * i + 1, s1_ref, j0)
@@ -391,10 +397,6 @@
     last = jnp.int32(g - 1)
     both(last - 1, s0_ref, last, s1_ref, 0)
     only_pv(last, s1_ref)
-    for gi in range(g - ML, g - 1):
-        merge_wait(gi)
-        merge(gi)
-        merge_send(gi)
     for gi in range(g - LAG, g - ML - 1):
         final_wait(gi)
         final(gi)

time: 56.4 us -> 55.9 us (level)
  no operation moved by 1% of the time
where the time goes in v6:
time: 55.9 us; the launch traced here: 55.8 us
  Pallas kernels  54 us (97%)
  local copies, waits for them, and re-layouts  1.83 us (3%)
    pallas_call x1, Pallas kernels, local(): pl.pallas_call(kernel, out_shape=jax.ShapeDtypeStruct((b, hl, lora), jnp....  54 us
    unnamed x1, local copies, waits for them, and re-layouts  1.83 us

profile of v6, /device:TPU:112, one launch (start us, length us, event | category | flops | bytes accessed | tf_op | source)
XLA Modules:
  0.0 55.8 jit_solution(10796643724448566642)
XLA Ops:
  0.0 54.0 %shard_map.37 = bf16[128,2,512]{2,1,0:T(2,128)(2,1)} custom-call(s32[128]{0:T(128)} %lens_hbm.1, bf16[2,576,128]{2,1,0:T(8,128)(2,1)} %bitcast.7, bf16[32,8,576,128]{3,2,1,0:T(8,128)(2,1)} %bitcast.6), custom_call_target="tpu_custom_call" | custom-call | tf_op jit(solution)/shard_map/pallas_call | solution.py:441
  54.0 1.8 %copy.6 = bf16[128,2,512]{2,1,0:T(2,128)(2,1)} copy(bf16[128,2,512]{2,1,0:T(2,128)(2,1)} %shard_map.37) | data formatting | bytes 524288
